TPU v7x, 128 devices: a whole 4x4x4 slice. The times are simulated.
128 devices in a mesh: gx: 8 (over z, core), gy: 16 (over y, x).
Axes of the slice: x: 4, y: 4, z: 4, core: 2. Of those that a mesh axis runs over, the one named last changes fastest.
Arguments:
- tables: float32 [2, 1048576, 128], P(None, ('gx', 'gy')), may hold values from -0.9 to 0.9
- cold_rows: int32 [128, 2, 128, 16], P(('gx', 'gy')), may hold values from 0 to 8191, as said below
- cold_bags: int32 [128, 2, 128, 16], P(('gx', 'gy')), may hold values from -1 to 127, as said below
- hot_rows: int32 [2, 256], replicated, may hold values from 0 to 1048575
- hot_ids: int32 [16384, 2, 8], P(('gx', 'gy')), may hold values from 0 to 255
Outputs:
- pooled: float32 [16384, 2, 128], P(('gx', 'gy'))
Inputs may be any that keep to these rules, and one draw needn't show every extreme that they name: `cold_rows`: every entry names one of the owner's 8192 rows. `cold_bags`: live slots of one sender, table and owner come first, the empty ones (-1) after them; in every draw each table has an owner whose 16 slots are all live from every sender.
All inputs are finite; a program needn't handle non-finite values.
Results may differ from a plain program's by a relative error of at most 0.0003.
Values sent between devices are 32-bit elements; how exact they have to be, the bound alone decides.
A program may use at most 64 MiB of HBM per device.

v0:
```python
import math

import jax
import jax.numpy as jnp
from jax import lax
from jax.sharding import Mesh
from jax.sharding import PartitionSpec as P

GX = ("gx_0", "gx_1")
GY = ("gy_0", "gy_1")
GX_GY = ("gx_0", "gx_1", "gy_0", "gy_1")


def padded_to(lines, count):
    spare = -len(lines) % count
    return jnp.pad(lines, [(0, spare)] + [(0, 0)] * (lines.ndim - 1))


def copy_for_each(x, axis):
    copies = jnp.broadcast_to(x, (lax.axis_size(axis), *x.shape))
    return lax.all_to_all(copies, axis, split_axis=0, concat_axis=0, tiled=True)


def in_order(tiles, dim):
    dims = list(tiles.shape[1:])
    dims[dim] *= tiles.shape[0]
    return jnp.moveaxis(tiles, 0, dim).reshape(dims)


def gather_axes(x, axes, dim):
    far, near = axes
    leading = copy_for_each(x, far)
    tiles = jnp.swapaxes(copy_for_each(leading, near), 0, 1)
    return in_order(tiles.reshape(-1, *x.shape), dim)


def in_blocks(x, dim, count):
    dims = x.shape
    tiles = x.reshape(*dims[:dim], count, dims[dim] // count, *dims[dim + 1 :])
    return jnp.moveaxis(tiles, dim, 0)


def sent_and_summed(x, axis, dim):
    count = lax.axis_size(axis)
    tiles = lax.all_to_all(in_blocks(x, dim, count), axis, 0, 0, tiled=True)
    return jnp.sum(tiles, axis=0)


def sum_by_axis(x, axes, dim):
    far, near = axes
    own = sent_and_summed(in_blocks(x, dim, lax.axis_size(far)), near, dim + 1)
    return jnp.sum(lax.all_to_all(own, far, 0, 0, tiled=True), axis=0)


def sum_by_parts(x, axes):
    lines = x.reshape(-1, x.shape[-1])
    padded = padded_to(lines, lax.axis_size(axes[0]) * lax.axis_size(axes[1]))
    whole = gather_axes(sum_by_axis(padded, axes, 0), axes, 0)
    return lax.slice_in_dim(whole, 0, len(lines)).reshape(x.shape)


def side_by_side(arrays, axis, split_dim, concat_dim, along):
    widths = [a.shape[along] for a in arrays]
    both = jnp.concatenate(arrays, axis=along)
    whole = lax.all_to_all(both, axis, split_axis=split_dim, concat_axis=concat_dim, tiled=True)
    return tuple(jnp.split(whole, [sum(widths[:k]) for k in range(1, len(widths))], axis=along))


def pick_rows(table, indices):
    count = indices.shape[0]
    block = math.gcd(512, count)
    row_ids = jnp.arange(table.shape[0], dtype=jnp.int32)
    grouped = indices.reshape(count // block, block)

    def one_block(wanted):
        selector = (wanted[:, None] == row_ids[None, :]).astype(jnp.float32)
        return jnp.dot(
            selector, table, precision=lax.Precision.HIGHEST, preferred_element_type=jnp.float32
        )

    return lax.map(one_block, grouped).reshape(count, table.shape[1])


def body(tables, cold_rows, cold_bags, hot_rows, hot_ids):
    axis_x = lax.axis_size(GX)
    axis_y = lax.axis_size(GY)
    peer_count = axis_x * axis_y
    table_count, rows_dev, emb_width = tables.shape
    slot_cap = cold_rows.shape[3]
    batch_rows = hot_ids.shape[0]
    hot_count = hot_rows.shape[1]
    my_index = lax.axis_index(GX_GY)
    hot_owner = hot_rows // rows_dev
    local_rows = jnp.where(hot_owner == my_index, hot_rows - my_index * rows_dev, -1)
    picked = jax.vmap(pick_rows)(tables, local_rows)
    hot_table = sum_by_parts(picked, (("gx_0", "gx_1", "gy_0"), "gy_1"))
    matches = jnp.sum(
        (
            hot_ids[:, :, :, None] == jnp.arange(hot_count, dtype=jnp.int32)[None, None, None, :]
        ).astype(jnp.float32),
        axis=2,
    )
    hot_part = jnp.einsum("bth,thd->btd", matches, hot_table, precision=lax.Precision.HIGHEST)
    my_rows = cold_rows[0]
    my_bags = cold_bags[0]
    got_rows, got_bags = side_by_side((my_rows, my_bags), GX_GY, 1, 1, 0)
    wanted_rows = jnp.where(got_bags >= 0, got_rows, -1)
    looked = jax.vmap(pick_rows)(tables, wanted_rows.reshape(table_count, -1))
    looked = looked.reshape(table_count, peer_count, slot_cap, emb_width)
    samples = jnp.arange(batch_rows, dtype=jnp.int32)
    returned = lax.all_to_all(looked, GX_GY, split_axis=1, concat_axis=1, tiled=True)
    onehot = (my_bags[:, None, :, :] == samples[None, :, None, None]).astype(jnp.float32)
    cold_part = jnp.einsum("tbpc,tpcd->btd", onehot, returned, precision=lax.Precision.HIGHEST)
    return cold_part + hot_part


def solution(mesh):
    finer = Mesh(mesh.devices.reshape(4, 2, 4, 4), ("gx_0", "gx_1", "gy_0", "gy_1"))
    return jax.shard_map(
        body,
        mesh=finer,
        in_specs=(
            P(None, GX_GY, None),
            P(GX_GY, None, None, None),
            P(GX_GY, None, None, None),
            P(),
            P(GX_GY, None, None),
        ),
        out_specs=P(GX_GY, None, None),
        check_vma=False,
    )
```

profile of v0, /device:TPU:1, one launch (start us, length us, event | category | flops | bytes accessed | tf_op | source)
XLA Modules:
  0.0 185.8 jit_solution(10558937564572457208)
XLA Ops:
  0.0 0.7 compare_select_fusion.1
  0.7 0.0 copy-start
  0.7 0.0 copy-start.1
  0.7 11.1 %fusion.6 = f32[2,256,128]{2,1,0:T(8,128)S(1)} fusion(f32[2,8192,128]{2,1,0:T(8,128)} %param.7, s32[2,256]{1,0:T(2,128)S(1)} %compare_select_fusion.1), kind=kOutput, calls=%fused_computation.9 | convolution fusion | flops 6446645248 | bytes 8652800 | tf_op jit(solution)/shard_map/vmap()/while/body/eval_jaxpr/dot_general | solution.py:77
  11.8 10.2 %all_to_all.30 = f32[4,32,4,128]{3,2,1,0:T(4,128)S(1)} all-to-all(f32[4,32,4,128]{3,2,1,0:T(4,128)S(1)} %bitcast.39), channel_id=1, replica_groups=mesh['gx_0'=4,'gx_1'=2,'gy_0'=4,'gy_1'=4] {'gy_1'}, dimensions={0} | all-to-all | bytes 524288 | tf_op jit(solution)/shard_map/all_to_all | solution.py:45
  22.0 0.7 reduce_sum.27
  22.7 10.2 %all-to-all-start.3 = ((f32[32,4,128]{2,1,0:T(4,128)}), f32[32,4,128]{2,1,0:T(4,128)S(1)}, u32[]{:S(2)}, u32[]{:S(2)}) async-start(f32[32,4,128]{2,1,0:T(4,128)} %reduce_sum.27), calls=%async_computation.3 | async-start | bytes 131072 | tf_op jit(solution)/shard_map/all_to_all | solution.py:52
  32.9 0.0 copy-done
  32.9 0.0 copy-done.1
  32.9 0.8 copy.51
  33.8 6.4 %all-to-all-done.3 = f32[32,4,128]{2,1,0:T(4,128)S(1)} async-done(((f32[32,4,128]{2,1,0:T(4,128)}), f32[32,4,128]{2,1,0:T(4,128)S(1)}, u32[]{:S(2)}, u32[]{:S(2)}) %all-to-all-start.3) | async-done | bytes 65568 | tf_op jit(solution)/shard_map/all_to_all | solution.py:52
  40.2 3.9 %all-to-all-start = ((s32[4,128,16]{2,0,1:T(4,128)}), s32[4,128,16]{2,0,1:T(4,128)S(1)}, u32[]{:S(2)}, u32[]{:S(2)}) async-start(s32[4,128,16]{2,0,1:T(4,128)} %copy.51), calls=%async_computation | async-start | bytes 524288 | tf_op jit(solution)/shard_map/all_to_all | solution.py:65
  44.2 11.2 %all-to-all-done = s32[4,128,16]{2,0,1:T(4,128)S(1)} async-done(((s32[4,128,16]{2,0,1:T(4,128)}), s32[4,128,16]{2,0,1:T(4,128)S(1)}, u32[]{:S(2)}, u32[]{:S(2)}) %all-to-all-start) | async-done | bytes 32800 | tf_op jit(solution)/shard_map/all_to_all | solution.py:65
  55.4 0.6 broadcast_in_dim.34
  56.0 4.2 %all-to-all-start.4 = ((f32[32,4,128]{2,1,0:T(4,128)}), f32[32,4,128]{2,1,0:T(4,128)S(1)}, u32[]{:S(2)}, u32[]{:S(2)}) async-start(f32[32,4,128]{2,1,0:T(4,128)} %broadcast_in_dim.34), calls=%async_computation.4 | async-start | bytes 131072 | tf_op jit(solution)/shard_map/all_to_all | solution.py:21
  60.2 0.1 compare_select_fusion
  60.3 0.1 reshape_reshape.6
  60.5 7.1 %all-to-all-done.4 = f32[32,4,128]{2,1,0:T(4,128)S(1)} async-done(((f32[32,4,128]{2,1,0:T(4,128)}), f32[32,4,128]{2,1,0:T(4,128)S(1)}, u32[]{:S(2)}, u32[]{:S(2)}) %all-to-all-start.4) | async-done | bytes 65568 | tf_op jit(solution)/shard_map/all_to_all | solution.py:21
  67.6 0.7 broadcast_in_dim.35
  68.3 3.6 %all-to-all-start.5 = ((f32[4,32,4,128]{3,2,1,0:T(4,128)}), f32[4,32,4,128]{3,2,1,0:T(4,128)S(1)}, u32[]{:S(2)}, u32[]{:S(2)}) async-start(f32[4,32,4,128]{3,2,1,0:T(4,128)} %broadcast_in_dim.35), calls=%async_computation.5 | async-start | bytes 524288 | tf_op jit(solution)/shard_map/all_to_all | solution.py:21
  71.9 72.4 %while.3 = (s32[]{:T(128)}, f32[4,2,512,128]{3,2,0,1:T(8,128)S(1)}, s32[4,2,512]{2,0,1:T(4,128)S(1)}, f32[2,8192,128]{2,1,0:T(8,128)}, s32[]{:T(128)}) while((s32[]{:T(128)}, f32[4,2,512,128]{3,2,0,1:T(8,128)S(1)}, s32[4,2,512]{2,0,1:T(4,128)S(1)}, f32[2,8192,128]{2,1,0:T(8,128)}, s32[]{:T(128)}) %tuple.31), condition=%wide.region_1.2_spmd.clone, body=%wide.region_0.1_spmd.clone.sunk | while | flops 12893290496 | bytes 8933453 | solution.py:81
  72.0 18.0 %fusion.20 = f32[4,2,512,128]{3,2,0,1:T(8,128)S(1)} fusion(f32[4,2,512,128]{3,2,0,1:T(8,128)S(1)} %get-tuple-element.117, s32[]{:T(128)S(6)} %copy.83, f32[2,8192,128]{2,1,0:T(8,128)} %get-tuple-element.124, s32[2,512]{1,0:T(2,128)S(1)} %bitcast.40), kind=kOutput, calls=%fused_computation.5.clone.1 | convolution fusion | flops 12893290496 | bytes 8916996 | tf_op jit(solution)/shard_map/vmap()/while/body/eval_jaxpr/dot_general | solution.py:77
  90.1 18.0 %fusion.20 = f32[4,2,512,128]{3,2,0,1:T(8,128)S(1)} fusion(f32[4,2,512,128]{3,2,0,1:T(8,128)S(1)} %get-tuple-element.117, s32[]{:T(128)S(6)} %copy.83, f32[2,8192,128]{2,1,0:T(8,128)} %get-tuple-element.124, s32[2,512]{1,0:T(2,128)S(1)} %bitcast.40), kind=kOutput, calls=%fused_computation.5.clone.1 | convolution fusion | flops 12893290496 | bytes 8916996 | tf_op jit(solution)/shard_map/vmap()/while/body/eval_jaxpr/dot_general | solution.py:77
  108.2 18.0 %fusion.20 = f32[4,2,512,128]{3,2,0,1:T(8,128)S(1)} fusion(f32[4,2,512,128]{3,2,0,1:T(8,128)S(1)} %get-tuple-element.117, s32[]{:T(128)S(6)} %copy.83, f32[2,8192,128]{2,1,0:T(8,128)} %get-tuple-element.124, s32[2,512]{1,0:T(2,128)S(1)} %bitcast.40), kind=kOutput, calls=%fused_computation.5.clone.1 | convolution fusion | flops 12893290496 | bytes 8916996 | tf_op jit(solution)/shard_map/vmap()/while/body/eval_jaxpr/dot_general | solution.py:77
  126.3 18.1 %fusion.20 = f32[4,2,512,128]{3,2,0,1:T(8,128)S(1)} fusion(f32[4,2,512,128]{3,2,0,1:T(8,128)S(1)} %get-tuple-element.117, s32[]{:T(128)S(6)} %copy.83, f32[2,8192,128]{2,1,0:T(8,128)} %get-tuple-element.124, s32[2,512]{1,0:T(2,128)S(1)} %bitcast.40), kind=kOutput, calls=%fused_computation.5.clone.1 | convolution fusion | flops 12893290496 | bytes 8916996 | tf_op jit(solution)/shard_map/vmap()/while/body/eval_jaxpr/dot_general | solution.py:77
  144.3 1.7 copy.55
  146.0 0.0 copy-start.2
  146.0 0.0 all-to-all-done.5
  146.0 6.1 %all-to-all-start.1 = ((f32[2,128,16,128]{3,2,0,1:T(8,128)}), f32[2,128,16,128]{3,2,0,1:T(8,128)S(1)}, u32[]{:S(2)}, u32[]{:S(2)}) async-start(f32[2,128,16,128]{3,2,0,1:T(8,128)} %copy.55), calls=%async_computation.1 | async-start | bytes 4194304 | tf_op jit(solution)/shard_map/all_to_all | solution.py:111
  152.1 0.1 copy.56
  152.2 0.0 copy-done.2
  152.2 0.1 copy.60
  152.3 0.8 convert_reduce_fusion
  153.2 28.5 %all-to-all-done.1 = f32[2,128,16,128]{3,2,0,1:T(8,128)S(1)} async-done(((f32[2,128,16,128]{3,2,0,1:T(8,128)}), f32[2,128,16,128]{3,2,0,1:T(8,128)S(1)}, u32[]{:S(2)}, u32[]{:S(2)}) %all-to-all-start.1) | async-done | bytes 2097184 | tf_op jit(solution)/shard_map/all_to_all | solution.py:111
  181.7 2.6 %fusion.10 = f32[2,128,128]{2,1,0:T(8,128)S(1)} fusion(f32[2,128,16,128]{3,2,0,1:T(8,128)S(1)} %all-to-all-done.1, s32[2,128,16]{2,0,1:T(2,128)S(1)} %copy.56), kind=kOutput, calls=%fused_computation.17 | convolution fusion | flops 805830656 | bytes 2244608 | tf_op jit(solution)/shard_map/tbpc,tpcd->btd/dot_general | solution.py:113
  184.4 0.6 fusion.9
  185.0 0.8 copy.63
  (14 shorter events, 0.2 us)
Async XLA Ops:
  0.7 32.2 %copy-start = (s32[1,2,128,16]{2,3,1,0:T(8,128)S(1)}, s32[1,2,128,16]{2,3,1,0:T(8,128)}, u32[]{:S(2)}) copy-start(s32[1,2,128,16]{2,3,1,0:T(8,128)} %param.9) | copy-start | bytes 49156
  0.7 32.2 %copy-start.1 = (s32[1,2,128,16]{2,3,1,0:T(8,128)S(1)}, s32[1,2,128,16]{2,3,1,0:T(8,128)}, u32[]{:S(2)}) copy-start(s32[1,2,128,16]{2,3,1,0:T(8,128)} %param.8) | copy-start | bytes 49156
  22.7 17.5 %all-to-all-start.3 = ((f32[32,4,128]{2,1,0:T(4,128)}), f32[32,4,128]{2,1,0:T(4,128)S(1)}, u32[]{:S(2)}, u32[]{:S(2)}) async-start(f32[32,4,128]{2,1,0:T(4,128)} %reduce_sum.27), calls=%async_computation.3 | async-start | bytes 131072 | tf_op jit(solution)/shard_map/all_to_all | solution.py:52
  40.2 15.2 %all-to-all-start = ((s32[4,128,16]{2,0,1:T(4,128)}), s32[4,128,16]{2,0,1:T(4,128)S(1)}, u32[]{:S(2)}, u32[]{:S(2)}) async-start(s32[4,128,16]{2,0,1:T(4,128)} %copy.51), calls=%async_computation | async-start | bytes 524288 | tf_op jit(solution)/shard_map/all_to_all | solution.py:65
  56.0 11.6 %all-to-all-start.4 = ((f32[32,4,128]{2,1,0:T(4,128)}), f32[32,4,128]{2,1,0:T(4,128)S(1)}, u32[]{:S(2)}, u32[]{:S(2)}) async-start(f32[32,4,128]{2,1,0:T(4,128)} %broadcast_in_dim.34), calls=%async_computation.4 | async-start | bytes 131072 | tf_op jit(solution)/shard_map/all_to_all | solution.py:21
  68.3 77.7 %all-to-all-start.5 = ((f32[4,32,4,128]{3,2,1,0:T(4,128)}), f32[4,32,4,128]{3,2,1,0:T(4,128)S(1)}, u32[]{:S(2)}, u32[]{:S(2)}) async-start(f32[4,32,4,128]{3,2,1,0:T(4,128)} %broadcast_in_dim.35), calls=%async_computation.5 | async-start | bytes 524288 | tf_op jit(solution)/shard_map/all_to_all | solution.py:21
  146.0 6.2 %copy-start.2 = (s32[128,2,8]{0,2,1:T(8,128)S(1)}, s32[128,2,8]{0,2,1:T(8,128)}, u32[]{:S(2)}) copy-start(s32[128,2,8]{0,2,1:T(8,128)} %param.11) | copy-start | bytes 24580
  146.0 35.7 %all-to-all-start.1 = ((f32[2,128,16,128]{3,2,0,1:T(8,128)}), f32[2,128,16,128]{3,2,0,1:T(8,128)S(1)}, u32[]{:S(2)}, u32[]{:S(2)}) async-start(f32[2,128,16,128]{3,2,0,1:T(8,128)} %copy.55), calls=%async_computation.1 | async-start | bytes 4194304 | tf_op jit(solution)/shard_map/all_to_all | solution.py:111
where the time goes:
time: 186 us
  matrix products  86.5 us (47%)
  waiting for transfers between devices  53.3 us (29%)
  starting transfers between devices  28 us (15%)
  blocking collectives  10.2 us (5%)
  local copies, waits for them, and re-layouts  5.18 us (3%)
  other arithmetic  2.34 us (1%)
    dot_general x5, matrix products, one_block(): jnp.dot(selector, table, precision=lax.Precision.HIGHEST, preferred_eleme...  83.3 us
    all_to_all x1, waiting for transfers between devices, body(): lax.all_to_all(looked, GX_GY, split_axis=1, concat_axis=1, tiled=True)  28.5 us
    all_to_all x1, waiting for transfers between devices, side_by_side(): lax.all_to_all(both, axis, split_axis=split_dim, concat_axis=concat_dim,...  11.2 us
    all_to_all x1, blocking collectives, sent_and_summed(): tiles = lax.all_to_all(in_blocks(x, dim, count), axis, 0, 0, tiled=True)  10.2 us
    all_to_all x1, starting transfers between devices, sum_by_axis(): return jnp.sum(lax.all_to_all(own, far, 0, 0, tiled=True), axis=0)  10.2 us
    all_to_all x2, starting transfers between devices, copy_for_each(): return lax.all_to_all(copies, axis, split_axis=0, concat_axis=0, tiled=True)  7.8 us
    all_to_all x2, waiting for transfers between devices, copy_for_each(): return lax.all_to_all(copies, axis, split_axis=0, concat_axis=0, tiled=True)  7.12 us
    all_to_all x1, waiting for transfers between devices, sum_by_axis(): return jnp.sum(lax.all_to_all(own, far, 0, 0, tiled=True), axis=0)  6.4 us
  transfers between devices with their start and end apart: 5, of which 4 were waited for; matrix products, arithmetic and copies ran while one was open for 41% of the time, Pallas kernels for 0%

commit v1 on v0

v1 whole, which is shorter than its diff:
```python
import functools

import jax
import jax.numpy as jnp
from jax import lax
from jax.experimental import pallas as pl
from jax.experimental.pallas import tpu as pltpu
from jax.sharding import PartitionSpec as P

MESH = pl.DeviceIdType.MESH
GX, GY = 8, 16
PEERS = GX * GY
CAP, TABLES, DIM = 16, 2, 128
ROWS_DEV, HOT, HOT_BAG, BATCH_DEV = 8192, 256, 8, 128
SLOTS = TABLES * CAP
STEP = 37


def split_bf16(x):
    high = x.astype(jnp.bfloat16)
    low = (x - high.astype(jnp.float32)).astype(jnp.bfloat16)
    return high, low


def kernel(
    tab_hbm, rows_hbm, bags_hbm, hot_rows_hbm, hot_ids_hbm, out_ref,
    tab, rows_v, bags_v, hot_rows_s, hot_ids_v, msg_t, idx_out, idx_in,
    bags_t, lanes, sbuf, rbuf, hot_own, hot_r1, hot_s1, hot_r2, hot_s2, hot_mine, hot_all, hot_flat,
    tab_sem, in_sems, idx_ssem, idx_rsem, self_sem, row_ssem, row_rsem,
    h_ssem, h_rsem,
):
    gx, gy = lax.axis_index("gx"), lax.axis_index("gy")
    me = gx * GY + gy
    z, core, y, x = gx // 2, gx % 2, gy // 4, gy % 4

    def peer(k):
        q = lax.rem(k * STEP, PEERS)
        px = lax.rem(z + q // 32, 4) * 2 + lax.rem(core + lax.rem(q // 16, 2), 2)
        py = lax.rem(y + lax.rem(q // 4, 4), 4) * 4 + lax.rem(x + lax.rem(q, 4), 4)
        return px, py

    barrier = pltpu.get_barrier_semaphore()

    def greet(k, carry):
        pl.semaphore_signal(barrier, inc=1, device_id=peer(k), device_id_type=MESH)
        return carry

    lax.fori_loop(1, PEERS, greet, 0)

    small = [
        pltpu.make_async_copy(rows_hbm, rows_v, in_sems.at[0]),
        pltpu.make_async_copy(hot_rows_hbm, hot_rows_s, in_sems.at[1]),
        pltpu.make_async_copy(bags_hbm, bags_v, in_sems.at[2]),
        pltpu.make_async_copy(hot_ids_hbm, hot_ids_v, in_sems.at[3]),
    ]
    for copy in small:
        copy.start()
    table_copy = pltpu.make_async_copy(tab_hbm, tab, tab_sem)
    table_copy.start()

    small[0].wait()
    padded = jnp.concatenate(
        [rows_v[...], jnp.zeros((PEERS - SLOTS, PEERS), jnp.int32)], axis=0
    )
    msg_t[...] = padded.T
    for p in range(PEERS):
        idx_out[p] = msg_t[pl.ds(p, 1), :]
    own_idx = pltpu.make_async_copy(idx_out.at[me], idx_in.at[me], self_sem)
    own_idx.start()

    small[1].wait()
    table_copy.wait()
    first = me * ROWS_DEV
    for t in range(TABLES):

        def pick_hot(i, carry, t=t):
            for j in range(4):
                local = hot_rows_s[t, i * 4 + j] - first
                mine = jnp.logical_and(local >= 0, local < ROWS_DEV)
                at = jnp.where(mine, local, 0)
                scale = jnp.where(mine, 1.0, 0.0)
                row = tab[t * ROWS_DEV + at]
                hot_own[t * 4 + i // 16, lax.rem(i, 16), pl.ds(j, 1), :] = row * scale
            return carry

        lax.fori_loop(0, HOT // 4, pick_hot, 0)

    pl.semaphore_wait(barrier, PEERS - 1)

    def send_idx(k, carry):
        px, py = peer(k)
        pltpu.make_async_remote_copy(
            src_ref=idx_out.at[px * GY + py], dst_ref=idx_in.at[me],
            send_sem=idx_ssem, recv_sem=idx_rsem.at[me],
            device_id=(px, py), device_id_type=MESH,
        ).start()
        return carry

    lax.fori_loop(1, PEERS, send_idx, 0)

    def gx_peer(k):
        return lax.rem(gx + k, GX)

    def gy_peer(k):
        return lax.rem(gy + k, GY)

    def hot_send(src, dst, stage, slot, device):
        pltpu.make_async_remote_copy(
            src_ref=src, dst_ref=dst, send_sem=h_ssem.at[stage], recv_sem=h_rsem.at[stage],
            device_id=device, device_id_type=MESH,
        ).start()

    def h_stage1(k, carry):
        d = gx_peer(k)
        hot_send(hot_own.at[d], hot_r1.at[k - 1], 0, 0, (d, gy))
        return carry

    lax.fori_loop(1, GX, h_stage1, 0)

    def drain(ref, sem):
        pltpu.make_async_copy(ref, ref, sem).wait()

    drain(hot_r1, h_rsem.at[0])
    total = hot_own[gx]
    for k in range(GX - 1):
        total = total + hot_r1[k]
    hot_s1[...] = total

    def h_stage2(k, carry):
        d = gy_peer(k)
        hot_send(hot_s1.at[d], hot_r2.at[k - 1], 1, 0, (gx, d))
        return carry

    lax.fori_loop(1, GY, h_stage2, 0)

    def fetch(p, put):
        for t in range(TABLES):
            for c in range(CAP):
                put(t * CAP + c, tab[t * ROWS_DEV + idx_in[p, 0, t * CAP + c]])

    def serve(k, carry):
        px, py = peer(k)
        p = px * GY + py
        drain(idx_in.at[p], idx_rsem.at[p])

        def put(slot, row):
            sbuf[k, pl.ds(slot, 1), :] = row

        fetch(p, put)
        pltpu.make_async_remote_copy(
            src_ref=sbuf.at[k], dst_ref=rbuf.at[me],
            send_sem=row_ssem, recv_sem=row_rsem,
            device_id=(px, py), device_id_type=MESH,
        ).start()
        return carry

    lax.fori_loop(1, 32, serve, 0)

    drain(hot_r2, h_rsem.at[1])
    total2 = hot_s1[gy]
    for k in range(GY - 1):
        total2 = total2 + hot_r2[k]
    hot_s2[...] = total2
    hot_mine[gy] = total2

    def h_stage3(k, carry):
        hot_send(hot_s2, hot_mine.at[gy], 2, 0, (gx, gy_peer(k)))
        return carry

    lax.fori_loop(1, GY, h_stage3, 0)

    lax.fori_loop(32, 64, serve, 0)

    drain(hot_r2, h_rsem.at[2])

    def h_stage4(k, carry):
        hot_send(hot_mine, hot_all.at[gx], 3, 0, (gx_peer(k), gy))
        return carry

    lax.fori_loop(1, GX, h_stage4, 0)
    hot_all[gx] = hot_mine[...]

    lax.fori_loop(64, PEERS, serve, 0)

    own_idx.wait()

    def put_own(slot, row):
        rbuf[me, pl.ds(slot, 1), :] = row

    fetch(me, put_own)

    small[2].wait()
    bags_t[...] = jnp.concatenate(
        [bags_v[...], jnp.zeros((PEERS - SLOTS, PEERS), jnp.int32)], axis=0
    ).T
    lane = lax.broadcasted_iota(jnp.int32, (CAP, PEERS), 1)
    for t in range(TABLES):
        line = jnp.zeros((CAP, PEERS), jnp.int32)
        for j in range(8):
            part = bags_t[pl.ds(j, 16, stride=8), :]
            moved = pltpu.roll(part, (j * CAP - t * CAP) % PEERS, axis=1)
            line = jnp.where(lane // CAP == j, moved, line)
        lanes[t] = line

    small[3].wait()
    drain(hot_r1, h_rsem.at[3])
    for b in range(GX):
        for g in range(GY):
            hot_flat[pl.ds((b * GY + g) * 4, 4), :] = hot_all[b, g]
    spot = lax.broadcasted_iota(jnp.int32, (HOT, BATCH_DEV), 0)
    sample = lax.broadcasted_iota(jnp.int32, (BATCH_DEV, 2 * PEERS), 0)
    parts = []
    for t in range(TABLES):
        counts = jnp.zeros((HOT, BATCH_DEV), jnp.float32)
        for k in range(HOT_BAG):
            ids = hot_ids_v[pl.ds(t * HOT_BAG + k, 1), :]
            counts = counts + jnp.where(ids == spot, 1.0, 0.0)
        counts = counts.T.astype(jnp.bfloat16)
        high, low = split_bf16(hot_flat[pl.ds(t * HOT, HOT), :])
        both = jnp.concatenate([high, low], axis=1)
        parts.append(jnp.dot(counts, both, preferred_element_type=jnp.float32))

    pltpu.make_async_copy(rbuf.at[pl.ds(0, PEERS - 1)], rbuf.at[pl.ds(0, PEERS - 1)], row_rsem).wait()
    for t in range(TABLES):
        acc = parts[t]
        for q in range(8):
            wanted = jnp.concatenate(
                [lanes[t, pl.ds(2 * q, 1), :], lanes[t, pl.ds(2 * q + 1, 1), :]], axis=1
            )
            onehot = jnp.where(wanted == sample, 1.0, 0.0).astype(jnp.bfloat16)
            rows = rbuf[pl.ds(q * 16, 16), pl.ds(t * CAP, CAP), :].reshape(256, DIM)
            high, low = split_bf16(rows)
            both = jnp.concatenate([high, low], axis=1)
            acc = acc + jnp.dot(onehot, both, preferred_element_type=jnp.float32)
        out_ref[pl.ds(t, BATCH_DEV, stride=2), :] = acc[:, :DIM] + acc[:, DIM:]

    drain(idx_out.at[pl.ds(0, PEERS - 1)], idx_ssem)
    drain(sbuf.at[pl.ds(0, PEERS - 1)], row_ssem)
    drain(hot_r1, h_ssem.at[0])
    drain(hot_r2, h_ssem.at[1])
    drain(hot_r2, h_ssem.at[2])
    drain(hot_r1, h_ssem.at[3])


def body(tables, cold_rows, cold_bags, hot_rows, hot_ids):
    tab = tables.reshape(TABLES * ROWS_DEV, 1, DIM)
    rows = cold_rows[0].transpose(0, 2, 1).reshape(SLOTS, PEERS)
    bags = cold_bags[0].transpose(0, 2, 1).reshape(SLOTS, PEERS)
    ids = hot_ids.transpose(1, 2, 0).reshape(TABLES * HOT_BAG, BATCH_DEV)
    f32, i32 = jnp.float32, jnp.int32
    out = pl.pallas_call(
        kernel,
        out_shape=jax.ShapeDtypeStruct((BATCH_DEV * TABLES, DIM), f32),
        in_specs=[pl.BlockSpec(memory_space=pl.ANY)] * 5,
        out_specs=pl.BlockSpec(memory_space=pltpu.VMEM),
        scratch_shapes=[
            pltpu.VMEM((TABLES * ROWS_DEV, 1, DIM), f32),
            pltpu.VMEM((SLOTS, PEERS), i32),
            pltpu.VMEM((SLOTS, PEERS), i32),
            pltpu.SMEM((TABLES, HOT), i32),
            pltpu.VMEM((TABLES * HOT_BAG, BATCH_DEV), i32),
            pltpu.VMEM((PEERS, PEERS), i32),
            pltpu.VMEM((PEERS, 1, PEERS), i32),
            pltpu.SMEM((PEERS, 1, PEERS), i32),
            pltpu.VMEM((PEERS, PEERS), i32),
            pltpu.VMEM((TABLES, CAP, PEERS), i32),
            pltpu.VMEM((PEERS, SLOTS, DIM), f32),
            pltpu.VMEM((PEERS, SLOTS, DIM), f32),
            pltpu.VMEM((GX, GY, 4, DIM), f32),
            pltpu.VMEM((GX - 1, GY, 4, DIM), f32),
            pltpu.VMEM((GY, 4, DIM), f32),
            pltpu.VMEM((GY - 1, 4, DIM), f32),
            pltpu.VMEM((4, DIM), f32),
            pltpu.VMEM((GY, 4, DIM), f32),
            pltpu.VMEM((GX, GY, 4, DIM), f32),
            pltpu.VMEM((TABLES * HOT, DIM), f32),
            pltpu.SemaphoreType.DMA,
            pltpu.SemaphoreType.DMA((4,)),
            pltpu.SemaphoreType.DMA,
            pltpu.SemaphoreType.DMA((PEERS,)),
            pltpu.SemaphoreType.DMA,
            pltpu.SemaphoreType.DMA,
            pltpu.SemaphoreType.DMA,
            pltpu.SemaphoreType.DMA((4,)),
            pltpu.SemaphoreType.DMA((4,)),
        ],
        compiler_params=pltpu.CompilerParams(
            collective_id=0, has_side_effects=True, vmem_limit_bytes=48 << 20
        ),
    )(tab, rows, bags, hot_rows, ids)
    return out.reshape(BATCH_DEV, TABLES, DIM)


def solution(mesh):
    both = ("gx", "gy")
    return jax.shard_map(
        body,
        mesh=mesh,
        in_specs=(
            P(None, both, None),
            P(both, None, None, None),
            P(both, None, None, None),
            P(),
            P(both, None, None),
        ),
        out_specs=P(both, None, None),
        check_vma=False,
    )
```

time: 186 us -> 61.6 us (0.33)
  matrix products: 86.5 us -> 0 us
  Pallas kernels: 0 us -> 57.7 us
  waiting for transfers between devices: 53.3 us -> 0 us
  starting transfers between devices: 28 us -> 0 us
  blocking collectives: 10.2 us -> 0 us
  other arithmetic: 2.34 us -> 0 us
    dot_general x7 -> x0, matrix products: 86.5 us -> none  [the longest x5 83.3 us: one_block(): jnp.dot(selector, table, precision=lax.Precision.HIGHEST, preferred_eleme...]
    pallas_call x0 -> x1, Pallas kernels: none -> 57.7 us  [body(): pl.pallas_call(kernel, out_shape=jax.ShapeDtypeStruct((BATCH_DEV * TABLES...]
    all_to_all x5 -> x0, waiting for transfers between devices: 53.3 us -> none  [the longest x1 28.5 us: body(): lax.all_to_all(looked, GX_GY, split_axis=1, concat_axis=1, tiled=True)]
    all_to_all x5 -> x0, starting transfers between devices: 28 us -> none  [the longest x1 10.2 us: sum_by_axis(): return jnp.sum(lax.all_to_all(own, far, 0, 0, tiled=True), axis=0)]
    all_to_all x1 -> x0, blocking collectives: 10.2 us -> none  [sent_and_summed(): tiles = lax.all_to_all(in_blocks(x, dim, count), axis, 0, 0, tiled=True)]
    unnamed x7 -> x9, local copies, waits for them, and re-layouts: 0.15 us -> 3.47 us
  transfers between devices with their start and end apart: 5 -> 0, of which waited for: 4 -> 0; matrix products, arithmetic and copies ran while one was open for 41% -> 0% of each run, Pallas kernels for 0% -> 0%
where the time goes in v1:
time: 61.6 us; the launch traced here: 61.2 us
  Pallas kernels  57.7 us (94%)
  local copies, waits for them, and re-layouts  3.47 us (6%)
    pallas_call x1, Pallas kernels, body(): pl.pallas_call(kernel, out_shape=jax.ShapeDtypeStruct((BATCH_DEV * TABLES...  57.7 us
    unnamed x9, local copies, waits for them, and re-layouts  3.47 us

profile of v1, /device:TPU:1, one launch (start us, length us, event | category | flops | bytes accessed | tf_op | source)
XLA Modules:
  0.0 61.2 jit_solution(4193702559008034490)
XLA Ops:
  0.0 0.0 copy-start
  0.0 0.7 %copy-done = s32[1,2,128,16]{2,3,1,0:T(8,128)S(1)} copy-done((s32[1,2,128,16]{2,3,1,0:T(8,128)S(1)}, s32[1,2,128,16]{2,3,1,0:T(8,128)}, u32[]{:S(2)}) %copy-start) | copy-done | bytes 16408
  0.7 0.0 copy-start.1
  0.7 0.7 %copy-done.1 = s32[1,2,128,16]{2,3,1,0:T(8,128)S(1)} copy-done((s32[1,2,128,16]{2,3,1,0:T(8,128)S(1)}, s32[1,2,128,16]{2,3,1,0:T(8,128)}, u32[]{:S(2)}) %copy-start.1) | copy-done | bytes 16408
  1.4 0.0 copy-start.2
  1.4 0.7 %copy-done.2 = s32[128,2,8]{0,2,1:T(8,128)S(1)} copy-done((s32[128,2,8]{0,2,1:T(8,128)S(1)}, s32[128,2,8]{0,2,1:T(8,128)}, u32[]{:S(2)}) %copy-start.2) | copy-done | bytes 8216
  2.1 0.0 copy-start.3
  2.1 0.7 %copy-done.3 = s32[2,256]{1,0:T(2,128)S(1)} copy-done((s32[2,256]{1,0:T(2,128)S(1)}, s32[2,256]{1,0:T(2,128)}, u32[]{:S(2)}) %copy-start.3) | copy-done | bytes 2072
  2.8 57.7 %shard_map.55 = f32[256,128]{1,0:T(8,128)S(1)} custom-call(f32[16384,1,128]{2,1,0:T(1,128)} %bitcast.19, s32[32,128]{1,0:T(8,128)S(1)} %bitcast.16, s32[32,128]{1,0:T(8,128)S(1)} %bitcast.17, s32[2,256]{1,0:T(2,128)S(1)} %copy-done.3, s32[16,128]{1,0:T(8,128)S(1)} %bitcast.18), custom_call_target="tpu_custom_call" | custom-call | tf_op jit(solution)/shard_map/pallas_call | solution.py:251
  60.6 0.7 %copy.7 = f32[128,2,128]{2,1,0:T(2,128)} copy(f32[128,2,128]{2,1,0:T(2,128)S(1)} %bitcast.15) | data formatting | bytes 262144
Async XLA Ops:
  0.0 0.7 %copy-start = (s32[1,2,128,16]{2,3,1,0:T(8,128)S(1)}, s32[1,2,128,16]{2,3,1,0:T(8,128)}, u32[]{:S(2)}) copy-start(s32[1,2,128,16]{2,3,1,0:T(8,128)} %param.6) | copy-start | bytes 49156
  0.7 0.7 %copy-start.1 = (s32[1,2,128,16]{2,3,1,0:T(8,128)S(1)}, s32[1,2,128,16]{2,3,1,0:T(8,128)}, u32[]{:S(2)}) copy-start(s32[1,2,128,16]{2,3,1,0:T(8,128)} %param.7) | copy-start | bytes 49156
  1.4 0.7 %copy-start.2 = (s32[128,2,8]{0,2,1:T(8,128)S(1)}, s32[128,2,8]{0,2,1:T(8,128)}, u32[]{:S(2)}) copy-start(s32[128,2,8]{0,2,1:T(8,128)} %param.9) | copy-start | bytes 24580
  2.1 0.7 %copy-start.3 = (s32[2,256]{1,0:T(2,128)S(1)}, s32[2,256]{1,0:T(2,128)}, u32[]{:S(2)}) copy-start(s32[2,256]{1,0:T(2,128)} %hot_rows_hbm.1) | copy-start | bytes 6148

commit v2 on v1

v2 whole, which is shorter than its diff:
```python
import jax
import jax.numpy as jnp
from jax import lax
from jax.experimental import pallas as pl
from jax.experimental.pallas import tpu as pltpu
from jax.sharding import PartitionSpec as P

MESH = pl.DeviceIdType.MESH
GX, GY = 8, 16
PEERS = GX * GY
CAP, TABLES, DIM = 16, 2, 128
ROWS_DEV, HOT, HOT_BAG, BATCH_DEV = 8192, 256, 8, 128
SLOTS = TABLES * CAP
ORDER = [
    (0, 0), (0, 1), (0, 3), (1, 0), (3, 0), (1, 1), (3, 3), (0, 2), (2, 0),
    (1, 3), (3, 1), (2, 2), (1, 2), (2, 3), (3, 2), (2, 1),
]


def split_bf16(x):
    high = x.astype(jnp.bfloat16)
    low = (x - high.astype(jnp.float32)).astype(jnp.bfloat16)
    return high, low


def kernel(
    tab_hbm, rows_hbm, bags_hbm, hot_rows_hbm, hot_ids_hbm, out_ref,
    tab, rows_v, bags_v, hot_rows_v, hot_at_v, hot_at, hot_ids_v, msg_t, idx_out, idx_mid, idx_in,
    bags_t, lanes, sbuf, rbuf, hot_own, hot_r1, hot_s1, hot_r2, hot_s2, hot_mine, hot_all, hot_flat,
    tab_sem, in_sems, at_sem, idx_ssem1, idx_rsem1, idx_ssem2, idx_rsem2, self_sem,
    row_ssem, row_rsem, h_ssem, h_rsem,
):
    gx, gy = lax.axis_index("gx"), lax.axis_index("gy")
    me = gx * GY + gy
    y, x = gy // 4, lax.rem(gy, 4)

    def gx_peer(k):
        return lax.rem(gx + k, GX)

    def gy_peer(dy, dx):
        return lax.rem(y + dy, 4) * 4 + lax.rem(x + dx, 4)

    cross = [gy_peer(dy, dx) for dy, dx in ORDER]
    ring = [gx_peer(k) for k in range(1, GX)]

    small = [
        pltpu.make_async_copy(rows_hbm, rows_v, in_sems.at[0]),
        pltpu.make_async_copy(hot_rows_hbm, hot_rows_v, in_sems.at[1]),
        pltpu.make_async_copy(bags_hbm, bags_v, in_sems.at[2]),
        pltpu.make_async_copy(hot_ids_hbm, hot_ids_v, in_sems.at[3]),
    ]
    small[0].start()

    barrier = pltpu.get_barrier_semaphore()
    for d in ring:
        pl.semaphore_signal(barrier, inc=1, device_id=(d, gy), device_id_type=MESH)
    for d in cross[1:]:
        pl.semaphore_signal(barrier, inc=1, device_id=(gx, d), device_id_type=MESH)

    for copy in small[1:]:
        copy.start()
    piece = TABLES * ROWS_DEV // 8
    for i in range(8):
        part = pl.ds(i * piece, piece)
        pltpu.make_async_copy(tab_hbm.at[part], tab.at[part], tab_sem).start()
    tab[TABLES * ROWS_DEV] = jnp.zeros((1, DIM), jnp.float32)

    small[1].wait()
    local = hot_rows_v[...] - me * ROWS_DEV
    mine = jnp.logical_and(local >= 0, local < ROWS_DEV)
    table = lax.broadcasted_iota(jnp.int32, (TABLES, HOT), 0)
    hot_at_v[...] = jnp.where(mine, local + table * ROWS_DEV, TABLES * ROWS_DEV)
    at_copy = pltpu.make_async_copy(hot_at_v, hot_at, at_sem)
    at_copy.start()

    small[0].wait()
    slot = lax.broadcasted_iota(jnp.int32, (SLOTS, PEERS), 0)
    padded = jnp.concatenate(
        [
            rows_v[...] + jnp.where(slot < CAP, 0, ROWS_DEV),
            jnp.zeros((PEERS - SLOTS, PEERS), jnp.int32),
        ],
        axis=0,
    )
    msg_t[...] = padded.T
    for p in range(PEERS):
        idx_out[p // GY, p % GY] = msg_t[pl.ds(p, 1), :]
    for g in range(GY):
        idx_mid[g, gx] = idx_out[gx, g]

    pl.semaphore_wait(barrier, GX + GY - 2)

    for d in ring:
        pltpu.make_async_remote_copy(
            src_ref=idx_out.at[d], dst_ref=idx_mid.at[:, gx],
            send_sem=idx_ssem1, recv_sem=idx_rsem1,
            device_id=(d, gy), device_id_type=MESH,
        ).start()

    def drain(ref, sem):
        pltpu.make_async_copy(ref, ref, sem).wait()

    def hot_send(src, dst, stage, device):
        pltpu.make_async_remote_copy(
            src_ref=src, dst_ref=dst, send_sem=h_ssem.at[stage], recv_sem=h_rsem.at[stage],
            device_id=device, device_id_type=MESH,
        ).start()

    at_copy.wait()
    drain(tab.at[pl.ds(0, TABLES * ROWS_DEV)], tab_sem)

    def pick_hot(i, carry):
        t, rest = i // GY, lax.rem(i, GY) * 16
        for j in range(16):
            row = tab[hot_at[t, rest + j]]
            hot_own[i // 4, lax.rem(i, 4) * 4 + j // 4, pl.ds(j % 4, 1), :] = row
        return carry

    lax.fori_loop(0, TABLES * HOT // 16, pick_hot, 0)
    for k, d in enumerate(ring):
        hot_send(hot_own.at[d], hot_r1.at[k], 0, (d, gy))

    drain(idx_mid.at[pl.ds(0, 14)], idx_rsem1)
    for d in cross[1:]:
        pltpu.make_async_remote_copy(
            src_ref=idx_mid.at[d], dst_ref=idx_in.at[gy],
            send_sem=idx_ssem2, recv_sem=idx_rsem2.at[gy],
            device_id=(gx, d), device_id_type=MESH,
        ).start()
    own_idx = pltpu.make_async_copy(idx_mid.at[gy], idx_in.at[gy], self_sem)
    own_idx.start()

    drain(hot_r1, h_rsem.at[0])
    total = hot_own[gx]
    for k in range(GX - 1):
        total = total + hot_r1[k]
    hot_s1[...] = total
    for k, d in enumerate(cross[1:]):
        hot_send(hot_s1.at[d], hot_r2.at[k], 1, (gx, d))

    def fetch(g, j, put):
        for slot in range(SLOTS):
            put(slot, tab[idx_in[g, j, 0, slot]])

    def serve(g, n):
        if n:
            drain(idx_in.at[g], idx_rsem2.at[g])
        else:
            own_idx.wait()

        def one(k, carry):
            d = gx_peer(k)

            def put(slot, row):
                sbuf[n * GX + k, pl.ds(slot, 1), :] = row

            fetch(g, d, put)
            pltpu.make_async_remote_copy(
                src_ref=sbuf.at[n * GX + k], dst_ref=rbuf.at[me],
                send_sem=row_ssem, recv_sem=row_rsem,
                device_id=(d, g), device_id_type=MESH,
            ).start()
            return carry

        lax.fori_loop(0 if n else 1, GX, one, 0)

    for n in range(0, 5):
        serve(cross[n], n)

    drain(hot_r2, h_rsem.at[1])
    total2 = hot_s1[gy]
    for k in range(GY - 1):
        total2 = total2 + hot_r2[k]
    hot_s2[...] = total2
    hot_mine[gy] = total2
    for d in cross[1:]:
        hot_send(hot_s2, hot_mine.at[gy], 2, (gx, d))

    for n in range(5, 10):
        serve(cross[n], n)

    drain(hot_r2, h_rsem.at[2])
    for d in ring:
        hot_send(hot_mine, hot_all.at[gx], 3, (d, gy))
    hot_all[gx] = hot_mine[...]

    for n in range(10, GY):
        serve(cross[n], n)

    def put_own(slot, row):
        rbuf[me, pl.ds(slot, 1), :] = row

    fetch(gy, gx, put_own)

    small[2].wait()
    bags_t[...] = jnp.concatenate(
        [bags_v[...], jnp.zeros((PEERS - SLOTS, PEERS), jnp.int32)], axis=0
    ).T
    lane = lax.broadcasted_iota(jnp.int32, (CAP, PEERS), 1)
    for t in range(TABLES):
        line = jnp.zeros((CAP, PEERS), jnp.int32)
        for j in range(8):
            part = bags_t[pl.ds(j, 16, stride=8), :]
            moved = pltpu.roll(part, (j * CAP - t * CAP) % PEERS, axis=1)
            line = jnp.where(lane // CAP == j, moved, line)
        lanes[t] = line

    small[3].wait()
    drain(hot_r1, h_rsem.at[3])
    for b in range(GX):
        for g in range(GY):
            hot_flat[pl.ds((b * GY + g) * 4, 4), :] = hot_all[b, g]
    spot = lax.broadcasted_iota(jnp.int32, (HOT, BATCH_DEV), 0)
    sample = lax.broadcasted_iota(jnp.int32, (BATCH_DEV, 2 * PEERS), 0)
    parts = []
    for t in range(TABLES):
        counts = jnp.zeros((HOT, BATCH_DEV), jnp.float32)
        for k in range(HOT_BAG):
            ids = hot_ids_v[pl.ds(t * HOT_BAG + k, 1), :]
            counts = counts + jnp.where(ids == spot, 1.0, 0.0)
        counts = counts.T.astype(jnp.bfloat16)
        high, low = split_bf16(hot_flat[pl.ds(t * HOT, HOT), :])
        both = jnp.concatenate([high, low], axis=1)
        parts.append(jnp.dot(counts, both, preferred_element_type=jnp.float32))

    drain(rbuf.at[pl.ds(0, PEERS - 1)], row_rsem)
    for t in range(TABLES):
        acc = parts[t]
        for q in range(8):
            wanted = jnp.concatenate(
                [lanes[t, pl.ds(2 * q, 1), :], lanes[t, pl.ds(2 * q + 1, 1), :]], axis=1
            )
            onehot = jnp.where(wanted == sample, 1.0, 0.0).astype(jnp.bfloat16)
            rows = rbuf[pl.ds(q * 16, 16), pl.ds(t * CAP, CAP), :].reshape(256, DIM)
            high, low = split_bf16(rows)
            both = jnp.concatenate([high, low], axis=1)
            acc = acc + jnp.dot(onehot, both, preferred_element_type=jnp.float32)
        out_ref[pl.ds(t, BATCH_DEV, stride=2), :] = acc[:, :DIM] + acc[:, DIM:]

    drain(idx_mid.at[pl.ds(0, 14)], idx_ssem1)
    drain(idx_mid.at[pl.ds(0, 15)], idx_ssem2)
    drain(sbuf.at[pl.ds(0, PEERS - 1)], row_ssem)
    drain(hot_r1, h_ssem.at[0])
    drain(hot_r2, h_ssem.at[1])
    drain(hot_r2, h_ssem.at[2])
    drain(hot_r1, h_ssem.at[3])


def body(tables, cold_rows, cold_bags, hot_rows, hot_ids):
    tab = tables.reshape(TABLES * ROWS_DEV, 1, DIM)
    rows = cold_rows[0].transpose(0, 2, 1).reshape(SLOTS, PEERS)
    bags = cold_bags[0].transpose(0, 2, 1).reshape(SLOTS, PEERS)
    ids = hot_ids.transpose(1, 2, 0).reshape(TABLES * HOT_BAG, BATCH_DEV)
    f32, i32 = jnp.float32, jnp.int32
    out = pl.pallas_call(
        kernel,
        out_shape=jax.ShapeDtypeStruct((BATCH_DEV * TABLES, DIM), f32),
        in_specs=[pl.BlockSpec(memory_space=pltpu.MemorySpace.HBM)] * 5,
        out_specs=pl.BlockSpec(memory_space=pltpu.VMEM),
        scratch_shapes=[
            pltpu.VMEM((TABLES * ROWS_DEV + 1, 1, DIM), f32),
            pltpu.VMEM((SLOTS, PEERS), i32),
            pltpu.VMEM((SLOTS, PEERS), i32),
            pltpu.VMEM((TABLES, HOT), i32),
            pltpu.VMEM((TABLES, HOT), i32),
            pltpu.SMEM((TABLES, HOT), i32),
            pltpu.VMEM((TABLES * HOT_BAG, BATCH_DEV), i32),
            pltpu.VMEM((PEERS, PEERS), i32),
            pltpu.VMEM((GX, GY, 1, PEERS), i32),
            pltpu.VMEM((GY, GX, 1, PEERS), i32),
            pltpu.SMEM((GY, GX, 1, PEERS), i32),
            pltpu.VMEM((PEERS, PEERS), i32),
            pltpu.VMEM((TABLES, CAP, PEERS), i32),
            pltpu.VMEM((PEERS, SLOTS, DIM), f32),
            pltpu.VMEM((PEERS, SLOTS, DIM), f32),
            pltpu.VMEM((GX, GY, 4, DIM), f32),
            pltpu.VMEM((GX - 1, GY, 4, DIM), f32),
            pltpu.VMEM((GY, 4, DIM), f32),
            pltpu.VMEM((GY - 1, 4, DIM), f32),
            pltpu.VMEM((4, DIM), f32),
            pltpu.VMEM((GY, 4, DIM), f32),
            pltpu.VMEM((GX, GY, 4, DIM), f32),
            pltpu.VMEM((TABLES * HOT, DIM), f32),
            pltpu.SemaphoreType.DMA,
            pltpu.SemaphoreType.DMA((4,)),
            pltpu.SemaphoreType.DMA,
            pltpu.SemaphoreType.DMA,
            pltpu.SemaphoreType.DMA,
            pltpu.SemaphoreType.DMA,
            pltpu.SemaphoreType.DMA((GY,)),
            pltpu.SemaphoreType.DMA,
            pltpu.SemaphoreType.DMA,
            pltpu.SemaphoreType.DMA,
            pltpu.SemaphoreType.DMA((4,)),
            pltpu.SemaphoreType.DMA((4,)),
        ],
        compiler_params=pltpu.CompilerParams(
            collective_id=0, has_side_effects=True, vmem_limit_bytes=48 << 20
        ),
    )(tab, rows, bags, hot_rows, ids)
    return out.reshape(BATCH_DEV, TABLES, DIM)


def solution(mesh):
    both = ("gx", "gy")
    return jax.shard_map(
        body,
        mesh=mesh,
        in_specs=(
            P(None, both, None),
            P(both, None, None, None),
            P(both, None, None, None),
            P(),
            P(both, None, None),
        ),
        out_specs=P(both, None, None),
        check_vma=False,
    )
```

time: 61.6 us -> 51.2 us (0.83)
  Pallas kernels: 57.7 us -> 47.1 us
    pallas_call x1, Pallas kernels: 57.7 us -> 47.1 us  [body(): pl.pallas_call(kernel, out_shape=jax.ShapeDtypeStruct((BATCH_DEV * TABLES...]
where the time goes in v2:
time: 51.2 us; the launch traced here: 50.6 us
  Pallas kernels  47.1 us (92%)
  local copies, waits for them, and re-layouts  3.47 us (7%)
    pallas_call x1, Pallas kernels, body(): pl.pallas_call(kernel, out_shape=jax.ShapeDtypeStruct((BATCH_DEV * TABLES...  47.1 us
    unnamed x9, local copies, waits for them, and re-layouts  3.47 us

profile of v2, /device:TPU:1, one launch (start us, length us, event | category | flops | bytes accessed | tf_op | source)
XLA Modules:
  0.0 50.6 jit_solution(4665644461005590953)
XLA Ops:
  0.0 0.0 copy-start
  0.0 0.7 %copy-done = s32[1,2,128,16]{2,3,1,0:T(8,128)S(1)} copy-done((s32[1,2,128,16]{2,3,1,0:T(8,128)S(1)}, s32[1,2,128,16]{2,3,1,0:T(8,128)}, u32[]{:S(2)}) %copy-start) | copy-done | bytes 16408
  0.7 0.0 copy-start.1
  0.7 0.7 %copy-done.1 = s32[1,2,128,16]{2,3,1,0:T(8,128)S(1)} copy-done((s32[1,2,128,16]{2,3,1,0:T(8,128)S(1)}, s32[1,2,128,16]{2,3,1,0:T(8,128)}, u32[]{:S(2)}) %copy-start.1) | copy-done | bytes 16408
  1.4 0.0 copy-start.2
  1.4 0.7 %copy-done.2 = s32[128,2,8]{0,2,1:T(8,128)S(1)} copy-done((s32[128,2,8]{0,2,1:T(8,128)S(1)}, s32[128,2,8]{0,2,1:T(8,128)}, u32[]{:S(2)}) %copy-start.2) | copy-done | bytes 8216
  2.1 0.0 copy-start.3
  2.1 0.7 %copy-done.3 = s32[2,256]{1,0:T(2,128)S(1)} copy-done((s32[2,256]{1,0:T(2,128)S(1)}, s32[2,256]{1,0:T(2,128)}, u32[]{:S(2)}) %copy-start.3) | copy-done | bytes 2072
  2.8 47.1 %shard_map.55 = f32[256,128]{1,0:T(8,128)S(1)} custom-call(f32[16384,1,128]{2,1,0:T(1,128)} %bitcast.19, s32[32,128]{1,0:T(8,128)S(1)} %bitcast.16, s32[32,128]{1,0:T(8,128)S(1)} %bitcast.17, s32[2,256]{1,0:T(2,128)S(1)} %copy-done.3, s32[16,128]{1,0:T(8,128)S(1)} %bitcast.18), custom_call_target="tpu_custom_call" | custom-call | tf_op jit(solution)/shard_map/pallas_call | solution.py:255
  50.0 0.7 %copy.7 = f32[128,2,128]{2,1,0:T(2,128)} copy(f32[128,2,128]{2,1,0:T(2,128)S(1)} %bitcast.15) | data formatting | bytes 262144
Async XLA Ops:
  0.0 0.7 %copy-start = (s32[1,2,128,16]{2,3,1,0:T(8,128)S(1)}, s32[1,2,128,16]{2,3,1,0:T(8,128)}, u32[]{:S(2)}) copy-start(s32[1,2,128,16]{2,3,1,0:T(8,128)} %param.6) | copy-start | bytes 49156
  0.7 0.7 %copy-start.1 = (s32[1,2,128,16]{2,3,1,0:T(8,128)S(1)}, s32[1,2,128,16]{2,3,1,0:T(8,128)}, u32[]{:S(2)}) copy-start(s32[1,2,128,16]{2,3,1,0:T(8,128)} %param.7) | copy-start | bytes 49156
  1.4 0.7 %copy-start.2 = (s32[128,2,8]{0,2,1:T(8,128)S(1)}, s32[128,2,8]{0,2,1:T(8,128)}, u32[]{:S(2)}) copy-start(s32[128,2,8]{0,2,1:T(8,128)} %param.9) | copy-start | bytes 24580
  2.1 0.7 %copy-start.3 = (s32[2,256]{1,0:T(2,128)S(1)}, s32[2,256]{1,0:T(2,128)}, u32[]{:S(2)}) copy-start(s32[2,256]{1,0:T(2,128)} %hot_rows_hbm.1) | copy-start | bytes 6148

commit v3 on v2

v3 whole, which is shorter than its diff:
```python
import jax
import jax.numpy as jnp
from jax import lax
from jax.experimental import pallas as pl
from jax.experimental.pallas import tpu as pltpu
from jax.sharding import PartitionSpec as P

MESH = pl.DeviceIdType.MESH
HBM = pltpu.MemorySpace.HBM
GX, GY = 8, 16
PEERS = GX * GY
CAP, TABLES, DIM = 16, 2, 128
ROWS_DEV, HOT, HOT_BAG, BATCH_DEV = 8192, 256, 8, 128
SLOTS = TABLES * CAP
STEP = 25
GROUP = 32
NEAR = 42
CORNERS = 54
CUTS = (6, 18)


def split_bf16(x):
    high = x.astype(jnp.bfloat16)
    low = (x - high.astype(jnp.float32)).astype(jnp.bfloat16)
    return high, low


def kernel(
    tab_hbm, rows_hbm, bags_hbm, hot_rows_hbm, hot_ids_hbm, out_ref,
    tab, rows_v, bags_v, hot_rows_v, hot_at_v, hot_at, hot_ids_v, msg_t, idx_out, idx_mid, idx_in, idx_near,
    bags_t, lanes, sbuf, rbuf, hot_own, hot_r0, hot_s0, hot_r1, hot_s1, hot_r2, hot_s2, hot_all,
    tab_sem, in_sems, at_sem, idx_ssem1, idx_rsem1, idx_ssem2, idx_rsem2, idx_csem, idx_crsem, self_sem,
    row_ssem, row_rsem, h_ssem, h_rsem,
):
    gx, gy = lax.axis_index("gx"), lax.axis_index("gy")
    me = gx * GY + gy
    y, x = gy // 4, lax.rem(gy, 4)
    z, core = gx // 2, lax.rem(gx, 2)

    def at(dz, dc, dy, dx):
        px = lax.rem(z + dz, 4) * 2 + lax.rem(core + dc, 2)
        return px, lax.rem(y + dy, 4) * 4 + lax.rem(x + dx, 4)

    group = [at(u // 8, u // 4 % 2, u % 4, 0) for u in range(1, GROUP)]
    near = [at(0, c // 4, c % 4, dx) for c in range(8) for dx in (1, 2, 3)]
    near += [at(dz, dc, 0, dx) for dz in (1, 2, 3) for dc in (0, 1) for dx in (1, 2, 3)]
    before = [at(dz, 0, dy, dx) for dz in (1, 2, 3) for dy in (1, 2, 3) for dx in (1, 3) if (dz + dy) % 2 != dx // 3]
    beside = [at(b // 4, 0, b % 4, 1 + (b + b // 4) % 2 * 2) for b in range(16)]
    along_x = [at(0, 0, 0, dx) for dx in (1, 2, 3)]

    def unit(px, py):
        return px * 4 + py // 4

    here = unit(gx, gy)
    block = z * 4 + y
    other = 1 - core
    partner = (z * 2 + other, gy)

    def drain(ref, sem):
        pltpu.make_async_copy(ref, ref, sem).wait()

    def hot_send(src, dst, stage, device):
        pltpu.make_async_remote_copy(
            src_ref=src, dst_ref=dst, send_sem=h_ssem.at[stage], recv_sem=h_rsem.at[stage],
            device_id=device, device_id_type=MESH,
        ).start()

    small = [
        pltpu.make_async_copy(rows_hbm, rows_v, in_sems.at[0]),
        pltpu.make_async_copy(hot_rows_hbm, hot_rows_v, in_sems.at[1]),
        pltpu.make_async_copy(bags_hbm, bags_v, in_sems.at[2]),
        pltpu.make_async_copy(hot_ids_hbm, hot_ids_v, in_sems.at[3]),
    ]
    for copy in small:
        copy.start()

    barrier = pltpu.get_barrier_semaphore()
    for device in before + near + group:
        pl.semaphore_signal(barrier, inc=1, device_id=device, device_id_type=MESH)
    tab[TABLES * ROWS_DEV] = jnp.zeros((1, DIM), jnp.float32)

    small[0].wait()
    piece = TABLES * ROWS_DEV // 8
    for i in range(8):
        part = pl.ds(i * piece, piece)
        pltpu.make_async_copy(tab_hbm.at[part], tab.at[part], tab_sem).start()
    slot = lax.broadcasted_iota(jnp.int32, (SLOTS, PEERS), 0)
    padded = jnp.concatenate(
        [
            rows_v[...] + jnp.where(slot < CAP, 0, ROWS_DEV),
            jnp.zeros((PEERS - SLOTS, PEERS), jnp.int32),
        ],
        axis=0,
    )
    msg_t[...] = padded.T
    for p in range(PEERS):
        idx_out[p] = msg_t[pl.ds(p, 1), :]
    for d in range(4):
        idx_mid[d, here] = idx_out[here * 4 + d]

    pl.semaphore_wait(barrier, len(before + near + group))

    for px, py in group:
        u = unit(px, py)
        pltpu.make_async_remote_copy(
            src_ref=idx_out.at[pl.ds(u * 4, 4)], dst_ref=idx_mid.at[:, here],
            send_sem=idx_ssem1, recv_sem=idx_rsem1,
            device_id=(px, py), device_id_type=MESH,
        ).start()
    for px, py in near:
        pltpu.make_async_remote_copy(
            src_ref=idx_out.at[px * GY + py], dst_ref=idx_near.at[me],
            send_sem=idx_csem, recv_sem=idx_crsem,
            device_id=(px, py), device_id_type=MESH,
        ).start()

    small[1].wait()
    local = hot_rows_v[...] - me * ROWS_DEV
    mine = jnp.logical_and(local >= 0, local < ROWS_DEV)
    table = lax.broadcasted_iota(jnp.int32, (TABLES, HOT), 0)
    hot_at_v[...] = jnp.where(mine, local + table * ROWS_DEV, TABLES * ROWS_DEV)
    at_copy = pltpu.make_async_copy(hot_at_v, hot_at, at_sem)
    at_copy.start()
    at_copy.wait()

    drain(tab.at[pl.ds(0, TABLES * ROWS_DEV)], tab_sem)

    def pick_hot(i, carry):
        t, block = i // 4, lax.rem(i, 4)
        for j in range(64):
            row = tab[hot_at[t, block * 64 + j]]
            hot_own[t, block * 4 + j // 16, pl.ds(j % 16, 1), :] = row
        return carry

    lax.fori_loop(0, TABLES * 4, pick_hot, 0)
    hot_send(hot_own.at[other], hot_r0, 0, partner)

    def serve(px, py, n, wanted):
        for slot in range(SLOTS):
            sbuf[n, pl.ds(slot, 1), :] = tab[wanted(px, py, slot)]
        pltpu.make_async_remote_copy(
            src_ref=sbuf.at[n], dst_ref=rbuf.at[me],
            send_sem=row_ssem, recv_sem=row_rsem,
            device_id=(px, py), device_id_type=MESH,
        ).start()

    def from_near(px, py, slot):
        return idx_near[px * GY + py, 0, slot]

    def from_far(px, py, slot):
        return idx_in[lax.rem(py, 4), unit(px, py), 0, slot]

    drain(hot_r0, h_rsem.at[0])
    hot_s0[...] = hot_own[core] + hot_r0[...]
    for px, py in beside:
        hot_send(hot_s0.at[px // 2 * 4 + py // 4], hot_r1.at[block], 1, (px, py))

    drain(idx_near.at[pl.ds(0, NEAR)], idx_crsem)
    for k, (c, dx) in enumerate([(6, 1), (7, 3), (6, 2), (7, 1), (6, 3), (7, 2)]):
        serve(*at(0, c // 4, c % 4, dx), 66 + k, from_near)

    pltpu.make_async_copy(idx_mid.at[:, pl.ds(0, GROUP - 1)], idx_mid.at[:, pl.ds(0, GROUP - 1)], idx_rsem1).wait()
    for device in along_x:
        pltpu.make_async_remote_copy(
            src_ref=idx_mid.at[lax.rem(device[1], 4)], dst_ref=idx_in.at[x],
            send_sem=idx_ssem2, recv_sem=idx_rsem2,
            device_id=device, device_id_type=MESH,
        ).start()
    own_idx = pltpu.make_async_copy(idx_mid.at[x], idx_in.at[x], self_sem)
    own_idx.start()

    own_idx.wait()

    def in_group(e):
        u = lax.rem(e * 11, GROUP)
        return at(u // 8, lax.rem(u // 4, 2), lax.rem(u, 4), 0)

    def serve_near(i, carry):
        n = i * 11
        for dx in (1, 2, 3):
            serve(*at(1 + i // 2, lax.rem(i, 2), 0, dx), n, from_near)
            serve(*at(0, i // 4, lax.rem(i, 4), 4 - dx), n + 1, from_near)
            serve(*in_group(i * 5 + dx), n + 2, from_far)
            n = n + 3
        serve(*in_group(i * 5 + 4), n, from_far)
        serve(*in_group(i * 5 + 5), n + 1, from_far)
        return carry

    lax.fori_loop(0, CUTS[0], serve_near, 0)

    drain(hot_r1, h_rsem.at[1])
    total = hot_r1[0]
    for k in range(1, 16):
        total = total + hot_r1[k]
    hot_s1[...] = total
    for k, device in enumerate(along_x):
        hot_send(hot_s1, hot_r2.at[k], 2, device)

    lax.fori_loop(CUTS[0], 6, serve_near, 0)
    serve(*in_group(31), 72, from_far)

    drain(idx_in.at[pl.ds(0, 3)], idx_rsem2)

    def serve_corner(k, carry):
        q = lax.rem(k * STEP, CORNERS)
        h = lax.rem(q, 9)
        device = at(1 + q // 18, lax.rem(q // 9, 2), 1 + h // 3, 1 + lax.rem(h, 3))
        serve(*device, PEERS - 1 - CORNERS + k, from_far)
        return carry

    lax.fori_loop(0, CUTS[1], serve_corner, 0)

    drain(hot_r2, h_rsem.at[2])
    total = (hot_s1[...] + hot_r2[0]) + (hot_r2[1] + hot_r2[2])
    hot_s2[...] = total
    hot_all[core, block] = total
    for device in beside[1:]:
        hot_send(hot_s2, hot_all.at[core, block], 3, device)

    lax.fori_loop(CUTS[1], CORNERS, serve_corner, 0)

    for slot in range(SLOTS):
        rbuf[me, pl.ds(slot, 1), :] = tab[idx_in[x, here, 0, slot]]

    small[2].wait()
    bags_t[...] = jnp.concatenate(
        [bags_v[...], jnp.zeros((PEERS - SLOTS, PEERS), jnp.int32)], axis=0
    ).T
    lane = lax.broadcasted_iota(jnp.int32, (CAP, PEERS), 1)
    for t in range(TABLES):
        line = jnp.zeros((CAP, PEERS), jnp.int32)
        for j in range(8):
            part = bags_t[pl.ds(j, 16, stride=8), :]
            moved = pltpu.roll(part, (j * CAP - t * CAP) % PEERS, axis=1)
            line = jnp.where(lane // CAP == j, moved, line)
        lanes[t] = line

    small[3].wait()
    drain(hot_r1.at[pl.ds(0, 15)], h_rsem.at[3])
    hot_send(hot_all.at[core], hot_all.at[core], 4, partner)

    drain(hot_r0, h_rsem.at[4])
    spot = lax.broadcasted_iota(jnp.int32, (HOT, BATCH_DEV), 0)
    sample = lax.broadcasted_iota(jnp.int32, (BATCH_DEV, 2 * PEERS), 0)
    parts = []
    for t in range(TABLES):
        counts = jnp.zeros((HOT, BATCH_DEV), jnp.float32)
        for k in range(HOT_BAG):
            ids = hot_ids_v[pl.ds(t * HOT_BAG + k, 1), :]
            counts = counts + jnp.where(ids == spot, 1.0, 0.0)
        counts = counts.T.astype(jnp.bfloat16)
        high, low = split_bf16(hot_all[t].reshape(HOT, DIM))
        both = jnp.concatenate([high, low], axis=1)
        parts.append(jnp.dot(counts, both, preferred_element_type=jnp.float32))

    drain(rbuf.at[pl.ds(0, PEERS - 1)], row_rsem)

    for t in range(TABLES):
        acc = parts[t]
        for q in range(8):
            wanted = jnp.concatenate(
                [lanes[t, pl.ds(2 * q, 1), :], lanes[t, pl.ds(2 * q + 1, 1), :]], axis=1
            )
            onehot = jnp.where(wanted == sample, 1.0, 0.0).astype(jnp.bfloat16)
            rows = rbuf[pl.ds(q * 16, 16), pl.ds(t * CAP, CAP), :].reshape(256, DIM)
            high, low = split_bf16(rows)
            both = jnp.concatenate([high, low], axis=1)
            acc = acc + jnp.dot(onehot, both, preferred_element_type=jnp.float32)
        out_ref[pl.ds(t, BATCH_DEV, stride=2), :] = acc[:, :DIM] + acc[:, DIM:]

    drain(idx_out.at[pl.ds(0, 4 * (GROUP - 1))], idx_ssem1)
    drain(idx_mid.at[pl.ds(0, 3)], idx_ssem2)
    drain(idx_near.at[pl.ds(0, NEAR)], idx_csem)
    drain(sbuf.at[pl.ds(0, PEERS - 1)], row_ssem)
    for stage, ref in enumerate((hot_r0, hot_r1, hot_r2, hot_r1.at[pl.ds(0, 15)], hot_r0)):
        drain(ref, h_ssem.at[stage])


def body(tables, cold_rows, cold_bags, hot_rows, hot_ids):
    tab = tables.reshape(TABLES * ROWS_DEV, 1, DIM)
    rows = cold_rows[0].transpose(0, 2, 1).reshape(SLOTS, PEERS)
    bags = cold_bags[0].transpose(0, 2, 1).reshape(SLOTS, PEERS)
    ids = hot_ids.transpose(1, 2, 0).reshape(TABLES * HOT_BAG, BATCH_DEV)
    f32, i32 = jnp.float32, jnp.int32
    out = pl.pallas_call(
        kernel,
        out_shape=jax.ShapeDtypeStruct((BATCH_DEV * TABLES, DIM), f32),
        in_specs=[pl.BlockSpec(memory_space=HBM)] * 5,
        out_specs=pl.BlockSpec(memory_space=pltpu.VMEM),
        scratch_shapes=[
            pltpu.VMEM((TABLES * ROWS_DEV + 1, 1, DIM), f32),
            pltpu.VMEM((SLOTS, PEERS), i32),
            pltpu.VMEM((SLOTS, PEERS), i32),
            pltpu.VMEM((TABLES, HOT), i32),
            pltpu.VMEM((TABLES, HOT), i32),
            pltpu.SMEM((TABLES, HOT), i32),
            pltpu.VMEM((TABLES * HOT_BAG, BATCH_DEV), i32),
            pltpu.VMEM((PEERS, PEERS), i32),
            pltpu.VMEM((PEERS, 1, PEERS), i32),
            pltpu.VMEM((4, GROUP, 1, PEERS), i32),
            pltpu.SMEM((4, GROUP, 1, PEERS), i32),
            pltpu.SMEM((PEERS, 1, PEERS), i32),
            pltpu.VMEM((PEERS, PEERS), i32),
            pltpu.VMEM((TABLES, CAP, PEERS), i32),
            pltpu.VMEM((PEERS, SLOTS, DIM), f32),
            pltpu.VMEM((PEERS, SLOTS, DIM), f32),
            pltpu.VMEM((TABLES, 16, 16, DIM), f32),
            pltpu.VMEM((16, 16, DIM), f32),
            pltpu.VMEM((16, 16, DIM), f32),
            pltpu.VMEM((16, 16, DIM), f32),
            pltpu.VMEM((16, DIM), f32),
            pltpu.VMEM((3, 16, DIM), f32),
            pltpu.VMEM((16, DIM), f32),
            pltpu.VMEM((TABLES, 16, 16, DIM), f32),
            pltpu.SemaphoreType.DMA,
            pltpu.SemaphoreType.DMA((4,)),
            pltpu.SemaphoreType.DMA,
            pltpu.SemaphoreType.DMA,
            pltpu.SemaphoreType.DMA,
            pltpu.SemaphoreType.DMA,
            pltpu.SemaphoreType.DMA,
            pltpu.SemaphoreType.DMA,
            pltpu.SemaphoreType.DMA,
            pltpu.SemaphoreType.DMA,
            pltpu.SemaphoreType.DMA,
            pltpu.SemaphoreType.DMA,
            pltpu.SemaphoreType.DMA((5,)),
            pltpu.SemaphoreType.DMA((5,)),
        ],
        compiler_params=pltpu.CompilerParams(
            collective_id=0, has_side_effects=True, vmem_limit_bytes=48 << 20
        ),
    )(tab, *(pltpu.with_memory_space_constraint(a, HBM) for a in (rows, bags, hot_rows, ids)))
    return out.reshape(BATCH_DEV, TABLES, DIM)


def solution(mesh):
    both = ("gx", "gy")
    return jax.shard_map(
        body,
        mesh=mesh,
        in_specs=(
            P(None, both, None),
            P(both, None, None, None),
            P(both, None, None, None),
            P(),
            P(both, None, None),
        ),
        out_specs=P(both, None, None),
        check_vma=False,
    )
```

time: 51.2 us -> 45.1 us (0.88)
  Pallas kernels: 47.1 us -> 44.2 us
  local copies, waits for them, and re-layouts: 3.47 us -> 0.66 us
    pallas_call x1, Pallas kernels: 47.1 us -> 44.2 us  [body(): pl.pallas_call(kernel, out_shape=jax.ShapeDtypeStruct((BATCH_DEV * TABLES...]
    unnamed x9 -> x1, local copies, waits for them, and re-layouts: 3.47 us -> 0.66 us
where the time goes in v3:
time: 45.1 us; the launch traced here: 44.9 us
  Pallas kernels  44.2 us (98%)
  local copies, waits for them, and re-layouts  0.66 us (1%)
    pallas_call x1, Pallas kernels, body(): pl.pallas_call(kernel, out_shape=jax.ShapeDtypeStruct((BATCH_DEV * TABLES...  44.2 us

profile of v3, /device:TPU:1, one launch (start us, length us, event | category | flops | bytes accessed | tf_op | source)
XLA Modules:
  0.0 44.9 jit_solution(15664366454765910393)
XLA Ops:
  0.0 44.2 %shard_map.55 = f32[256,128]{1,0:T(8,128)S(1)} custom-call(f32[16384,1,128]{2,1,0:T(1,128)} %bitcast.16, s32[32,128]{1,0:T(8,128)} %bitcast.17, s32[32,128]{1,0:T(8,128)} %bitcast.18, s32[2,256]{1,0:T(2,128)} %hot_rows_hbm.1, s32[16,128]{1,0:T(8,128)} %bitcast.19), custom_call_target="tpu_custom_call" | custom-call | tf_op jit(solution)/shard_map/pallas_call | solution.py:285
  44.3 0.7 %copy.7 = f32[128,2,128]{2,1,0:T(2,128)} copy(f32[128,2,128]{2,1,0:T(2,128)S(1)} %bitcast.15) | data formatting | bytes 262144

commit v4 on v3

v4 whole, which is shorter than its diff:
```python
import jax
import jax.numpy as jnp
from jax import lax
from jax.experimental import pallas as pl
from jax.experimental.pallas import tpu as pltpu
from jax.sharding import PartitionSpec as P

MESH = pl.DeviceIdType.MESH
HBM = pltpu.MemorySpace.HBM
GX, GY = 8, 16
PEERS = GX * GY
CAP, TABLES, DIM = 16, 2, 128
ROWS_DEV, HOT, HOT_BAG, BATCH_DEV = 8192, 256, 8, 128
SLOTS = TABLES * CAP
GROUP = 32
CUTS = (60, 90)


def hops(offset):
    dz, _, dy, dx = offset
    return sum(min(d, 4 - d) for d in (dz, dy, dx))


def neg(offset):
    dz, dc, dy, dx = offset
    return -dz % 4, dc, -dy % 4, -dx % 4


LINE = [(0, dc, 0, dx) for dx in (1, 3, 2) for dc in (0, 1)]
NEAR = [(0, dc, dy, dx) for dc in (0, 1) for dy in (1, 2, 3) for dx in (1, 2, 3)]
NEAR += [(dz, dc, 0, dx) for dz in (1, 2, 3) for dc in (0, 1) for dx in (1, 2, 3)]

ACROSS = [(u // 8, u // 4 % 2, u % 4, 0) for u in range(1, GROUP)]
BEFORE = [(dz, 0, dy, dx) for dz in (1, 2, 3) for dy in (1, 2, 3) for dx in (1, 3) if (dz + dy) % 2 != dx // 3]


def orders():
    every = [(q // 32, q // 16 % 2, q // 4 % 4, q % 4) for q in (k * STEP % PEERS for k in range(1, PEERS))]
    last = [o for o in every if hops(o) <= LAST]
    corners = [o for o in every if o[0] and o[2] and o[3]]
    planes = [o for o in every if o not in last and o not in corners]
    return planes, corners, last


STEP, LAST = 79, 1


def split_bf16(x):
    high = x.astype(jnp.bfloat16)
    low = (x - high.astype(jnp.float32)).astype(jnp.bfloat16)
    return high, low


def kernel(
    tab_hbm, rows_hbm, bags_hbm, hot_rows_hbm, hot_ids_hbm, out_ref,
    tab, rows_v, bags_v, hot_rows_v, hot_at_v, hot_at, hot_ids_v, msg_t, idx_out, idx_mid, idx_line, idx_near, idx_far, idx_own,
    bags_t, bags_p, lanes, sbuf, rbuf, hot_own, hot_r0, hot_s0, hot_r1, hot_s1, hot_r2, hot_s2, hot_in, hot_pin, hot_ps, hot_all,
    tab_sem, in_sems, at_sem, idx_ssem1, idx_rsem1, idx_ssem2, idx_rsem2, idx_csem, idx_crsem, self_sem,
    row_ssem, row_rsem, h_ssem, h_rsem,
):
    gx, gy = lax.axis_index("gx"), lax.axis_index("gy")
    me = gx * GY + gy
    y, x = gy // 4, lax.rem(gy, 4)
    z, core = gx // 2, lax.rem(gx, 2)

    def at(dz, dc, dy, dx):
        px = lax.rem(z + dz, 4) * 2 + lax.rem(core + dc, 2)
        return px, lax.rem(y + dy, 4) * 4 + lax.rem(x + dx, 4)

    known = [at(*o) for o in sorted(BEFORE + NEAR + ACROSS + LINE, key=hops, reverse=True)]
    beside = [at(b // 4, 0, b % 4, 1 + (b + b // 4) % 2 * 2) for b in range(16)]
    along_x = [at(0, 0, 0, dx) for dx in (1, 2, 3)]

    def unit(px, py):
        return px * 4 + py // 4

    here = unit(gx, gy)
    block = z * 4 + y
    other = 1 - core
    partner = (z * 2 + other, gy)

    def drain(ref, sem):
        pltpu.make_async_copy(ref, ref, sem).wait()

    def hot_send(src, dst, stage, device):
        pltpu.make_async_remote_copy(
            src_ref=src, dst_ref=dst, send_sem=h_ssem.at[stage], recv_sem=h_rsem.at[stage],
            device_id=device, device_id_type=MESH,
        ).start()

    small = [
        pltpu.make_async_copy(rows_hbm, rows_v, in_sems.at[0]),
        pltpu.make_async_copy(hot_rows_hbm, hot_rows_v, in_sems.at[1]),
        pltpu.make_async_copy(bags_hbm, bags_v, in_sems.at[2]),
        pltpu.make_async_copy(hot_ids_hbm, hot_ids_v, in_sems.at[3]),
    ]
    for copy in small:
        copy.start()

    barrier = pltpu.get_barrier_semaphore()
    for device in known:
        pl.semaphore_signal(barrier, inc=1, device_id=device, device_id_type=MESH)
    tab[TABLES * ROWS_DEV] = jnp.zeros((1, DIM), jnp.float32)

    small[0].wait()
    piece = TABLES * ROWS_DEV // 8
    for i in range(8):
        part = pl.ds(i * piece, piece)
        pltpu.make_async_copy(tab_hbm.at[part], tab.at[part], tab_sem).start()
    slot = lax.broadcasted_iota(jnp.int32, (SLOTS, PEERS), 0)
    padded = jnp.concatenate(
        [
            rows_v[...] + jnp.where(slot < CAP, 0, ROWS_DEV),
            jnp.zeros((PEERS - SLOTS, PEERS), jnp.int32),
        ],
        axis=0,
    )
    msg_t[...] = padded.T
    for p in range(PEERS):
        idx_out[p] = msg_t[pl.ds(p, 1), :]
    for d in range(4):
        idx_mid[d, here] = idx_out[here * 4 + d]

    pl.semaphore_wait(barrier, len(known))

    def tell(o, landing, kind):
        px, py = at(*o)
        pltpu.make_async_remote_copy(
            src_ref=idx_out.at[px * GY + py], dst_ref=landing,
            send_sem=idx_csem, recv_sem=idx_crsem.at[kind],
            device_id=(px, py), device_id_type=MESH,
        ).start()

    def tell_group(o):
        px, py = at(*o)
        pltpu.make_async_remote_copy(
            src_ref=idx_out.at[pl.ds(unit(px, py) * 4, 4)], dst_ref=idx_mid.at[:, here],
            send_sem=idx_ssem1, recv_sem=idx_rsem1,
            device_id=(px, py), device_id_type=MESH,
        ).start()

    for o in sorted(NEAR + ACROSS + LINE, key=hops, reverse=True):
        if o in LINE:
            tell(o, idx_line.at[LINE.index(o)], 0)
        elif o in NEAR:
            tell(o, idx_near.at[NEAR.index(o)], 1)
        else:
            tell_group(o)

    small[1].wait()
    local = hot_rows_v[...] - me * ROWS_DEV
    mine = jnp.logical_and(local >= 0, local < ROWS_DEV)
    table = lax.broadcasted_iota(jnp.int32, (TABLES, HOT), 0)
    hot_at_v[...] = jnp.where(mine, local + table * ROWS_DEV, TABLES * ROWS_DEV)
    at_copy = pltpu.make_async_copy(hot_at_v, hot_at, at_sem)
    at_copy.start()
    at_copy.wait()

    drain(tab.at[pl.ds(0, TABLES * ROWS_DEV)], tab_sem)

    for t in range(TABLES):
        for h in range(HOT):
            hot_own[t, h // 16, pl.ds(h % 16, 1), :] = tab[hot_at[t, h]]
    hot_send(hot_own.at[other], hot_r0, 0, partner)

    planes, corners, last = orders()
    sequence = planes + corners + last

    def serve(first, stop):
        for n in range(first, stop):
            o = sequence[n]
            px, py = at(*o)
            u = unit(px, py)
            if o in LINE:
                asked = [idx_line[LINE.index(neg(o)), 0, slot] for slot in range(SLOTS)]
            elif o in NEAR:
                asked = [idx_near[NEAR.index(neg(o)), 0, slot] for slot in range(SLOTS)]
            elif o[3]:
                asked = [idx_far[3 - o[3], u, 0, slot] for slot in range(SLOTS)]
            else:
                asked = [idx_own[u, 0, slot] for slot in range(SLOTS)]
            for slot in range(SLOTS):
                sbuf[n, pl.ds(slot, 1), :] = tab[asked[slot]]
            pltpu.make_async_remote_copy(
                src_ref=sbuf.at[n], dst_ref=rbuf.at[n],
                send_sem=row_ssem, recv_sem=row_rsem.at[n // 16],
                device_id=(px, py), device_id_type=MESH,
            ).start()

    drain(hot_r0, h_rsem.at[0])
    hot_s0[...] = hot_own[core] + hot_r0[...]
    for px, py in beside:
        hot_send(hot_s0.at[px // 2 * 4 + py // 4], hot_r1.at[block], 1, (px, py))

    drain(idx_line, idx_crsem.at[0])
    drain(idx_near, idx_crsem.at[1])

    pltpu.make_async_copy(idx_mid.at[:, pl.ds(0, GROUP - 1)], idx_mid.at[:, pl.ds(0, GROUP - 1)], idx_rsem1).wait()
    for k, device in enumerate(along_x):
        pltpu.make_async_remote_copy(
            src_ref=idx_mid.at[lax.rem(device[1], 4)], dst_ref=idx_far.at[k],
            send_sem=idx_ssem2, recv_sem=idx_rsem2,
            device_id=device, device_id_type=MESH,
        ).start()
    own_idx = pltpu.make_async_copy(idx_mid.at[x], idx_own, self_sem)
    own_idx.start()

    own_idx.wait()

    serve(0, min(CUTS[0], len(planes)))

    drain(hot_r1, h_rsem.at[1])
    total = hot_r1[0]
    for k in range(1, 16):
        total = total + hot_r1[k]
    hot_s1[...] = total
    for k, device in enumerate(along_x):
        hot_send(hot_s1, hot_r2.at[k], 2, device)

    serve(min(CUTS[0], len(planes)), len(planes))

    drain(idx_far, idx_rsem2)

    serve(len(planes), max(CUTS[1], len(planes)))

    drain(hot_r2, h_rsem.at[2])
    total = (hot_s1[...] + hot_r2[0]) + (hot_r2[1] + hot_r2[2])
    hot_s2[...] = total
    for k, device in enumerate(beside[1:]):
        hot_send(hot_s2, hot_in.at[k], 3, device)

    serve(max(CUTS[1], len(planes)), PEERS - 1)

    for slot in range(SLOTS):
        rbuf[PEERS - 1, pl.ds(slot, 1), :] = tab[idx_own[here, 0, slot]]

    small[2].wait()
    bags_t[...] = jnp.concatenate(
        [bags_v[...], jnp.zeros((PEERS - SLOTS, PEERS), jnp.int32)], axis=0
    ).T
    for p in range(PEERS):
        bags_p[p] = bags_t[pl.ds(p, 1), :]
    for n, (dz, dc, dy, dx) in enumerate(sequence + [(0, 0, 0, 0)]):
        px, py = at(*neg((dz, dc, dy, dx)))
        bags_t[pl.ds(n, 1), :] = bags_p[px * GY + py]
    lane = lax.broadcasted_iota(jnp.int32, (CAP, PEERS), 1)
    for t in range(TABLES):
        line = jnp.zeros((CAP, PEERS), jnp.int32)
        for j in range(8):
            part = bags_t[pl.ds(j, 16, stride=8), :]
            moved = pltpu.roll(part, (j * CAP - t * CAP) % PEERS, axis=1)
            line = jnp.where(lane // CAP == j, moved, line)
        lanes[t] = line

    small[3].wait()
    drain(hot_in, h_rsem.at[3])
    hot_send(hot_in, hot_pin, 4, partner)
    hot_send(hot_s2, hot_ps, 5, partner)

    drain(hot_pin, h_rsem.at[4])
    drain(hot_ps, h_rsem.at[5])
    hot_all[core, block] = hot_s2[...]
    hot_all[other, block] = hot_ps[...]
    for b in range(1, 16):
        from_b = lax.rem(z + 4 - b // 4, 4) * 4 + lax.rem(y + 4 - b % 4, 4)
        hot_all[core, from_b] = hot_in[b - 1]
        hot_all[other, from_b] = hot_pin[b - 1]
    spot = lax.broadcasted_iota(jnp.int32, (HOT, BATCH_DEV), 0)
    sample = lax.broadcasted_iota(jnp.int32, (BATCH_DEV, 2 * PEERS), 0)
    parts = []
    for t in range(TABLES):
        counts = jnp.zeros((HOT, BATCH_DEV), jnp.float32)
        for k in range(HOT_BAG):
            ids = hot_ids_v[pl.ds(t * HOT_BAG + k, 1), :]
            counts = counts + jnp.where(ids == spot, 1.0, 0.0)
        counts = counts.T.astype(jnp.bfloat16)
        high, low = split_bf16(hot_all[t].reshape(HOT, DIM))
        both = jnp.concatenate([high, low], axis=1)
        parts.append(jnp.dot(counts, both, preferred_element_type=jnp.float32))

    for q in range(8):
        drain(rbuf.at[pl.ds(q * 16, 16 if q < 7 else 15)], row_rsem.at[q])
        for t in range(TABLES):
            wanted = jnp.concatenate(
                [lanes[t, pl.ds(2 * q, 1), :], lanes[t, pl.ds(2 * q + 1, 1), :]], axis=1
            )
            onehot = jnp.where(wanted == sample, 1.0, 0.0).astype(jnp.bfloat16)
            rows = rbuf[pl.ds(q * 16, 16), pl.ds(t * CAP, CAP), :].reshape(256, DIM)
            high, low = split_bf16(rows)
            both = jnp.concatenate([high, low], axis=1)
            parts[t] = parts[t] + jnp.dot(onehot, both, preferred_element_type=jnp.float32)
    for t in range(TABLES):
        out_ref[pl.ds(t, BATCH_DEV, stride=2), :] = parts[t][:, :DIM] + parts[t][:, DIM:]

    drain(idx_out.at[pl.ds(0, 4 * (GROUP - 1))], idx_ssem1)
    drain(idx_far, idx_ssem2)
    drain(idx_out.at[pl.ds(0, len(LINE + NEAR))], idx_csem)
    drain(sbuf.at[pl.ds(0, PEERS - 1)], row_ssem)
    for stage, ref in enumerate((hot_r0, hot_r1, hot_r2, hot_in, hot_pin, hot_ps)):
        drain(ref, h_ssem.at[stage])


def body(tables, cold_rows, cold_bags, hot_rows, hot_ids):
    tab = tables.reshape(TABLES * ROWS_DEV, 1, DIM)
    rows = cold_rows[0].transpose(0, 2, 1).reshape(SLOTS, PEERS)
    bags = cold_bags[0].transpose(0, 2, 1).reshape(SLOTS, PEERS)
    ids = hot_ids.transpose(1, 2, 0).reshape(TABLES * HOT_BAG, BATCH_DEV)
    f32, i32 = jnp.float32, jnp.int32
    out = pl.pallas_call(
        kernel,
        out_shape=jax.ShapeDtypeStruct((BATCH_DEV * TABLES, DIM), f32),
        in_specs=[pl.BlockSpec(memory_space=HBM)] * 5,
        out_specs=pl.BlockSpec(memory_space=pltpu.VMEM),
        scratch_shapes=[
            pltpu.VMEM((TABLES * ROWS_DEV + 1, 1, DIM), f32),
            pltpu.VMEM((SLOTS, PEERS), i32),
            pltpu.VMEM((SLOTS, PEERS), i32),
            pltpu.VMEM((TABLES, HOT), i32),
            pltpu.VMEM((TABLES, HOT), i32),
            pltpu.SMEM((TABLES, HOT), i32),
            pltpu.VMEM((TABLES * HOT_BAG, BATCH_DEV), i32),
            pltpu.VMEM((PEERS, PEERS), i32),
            pltpu.VMEM((PEERS, 1, PEERS), i32),
            pltpu.VMEM((4, GROUP, 1, PEERS), i32),
            pltpu.SMEM((len(LINE), 1, PEERS), i32),
            pltpu.SMEM((len(NEAR), 1, PEERS), i32),
            pltpu.SMEM((3, GROUP, 1, PEERS), i32),
            pltpu.SMEM((GROUP, 1, PEERS), i32),
            pltpu.VMEM((PEERS, PEERS), i32),
            pltpu.VMEM((PEERS, 1, PEERS), i32),
            pltpu.VMEM((TABLES, CAP, PEERS), i32),
            pltpu.VMEM((PEERS, SLOTS, DIM), f32),
            pltpu.VMEM((PEERS, SLOTS, DIM), f32),
            pltpu.VMEM((TABLES, 16, 16, DIM), f32),
            pltpu.VMEM((16, 16, DIM), f32),
            pltpu.VMEM((16, 16, DIM), f32),
            pltpu.VMEM((16, 16, DIM), f32),
            pltpu.VMEM((16, DIM), f32),
            pltpu.VMEM((3, 16, DIM), f32),
            pltpu.VMEM((16, DIM), f32),
            pltpu.VMEM((15, 16, DIM), f32),
            pltpu.VMEM((15, 16, DIM), f32),
            pltpu.VMEM((16, DIM), f32),
            pltpu.VMEM((TABLES, 16, 16, DIM), f32),
            pltpu.SemaphoreType.DMA,
            pltpu.SemaphoreType.DMA((4,)),
            pltpu.SemaphoreType.DMA,
            pltpu.SemaphoreType.DMA,
            pltpu.SemaphoreType.DMA,
            pltpu.SemaphoreType.DMA,
            pltpu.SemaphoreType.DMA,
            pltpu.SemaphoreType.DMA,
            pltpu.SemaphoreType.DMA((2,)),
            pltpu.SemaphoreType.DMA,
            pltpu.SemaphoreType.DMA,
            pltpu.SemaphoreType.DMA((8,)),
            pltpu.SemaphoreType.DMA((6,)),
            pltpu.SemaphoreType.DMA((6,)),
        ],
        compiler_params=pltpu.CompilerParams(
            collective_id=0, has_side_effects=True, vmem_limit_bytes=48 << 20
        ),
    )(tab, *(pltpu.with_memory_space_constraint(a, HBM) for a in (rows, bags, hot_rows, ids)))
    return out.reshape(BATCH_DEV, TABLES, DIM)


def solution(mesh):
    both = ("gx", "gy")
    return jax.shard_map(
        body,
        mesh=mesh,
        in_specs=(
            P(None, both, None),
            P(both, None, None, None),
            P(both, None, None, None),
            P(),
            P(both, None, None),
        ),
        out_specs=P(both, None, None),
        check_vma=False,
    )
```

time: 45.1 us -> 44.4 us (0.984)
  Pallas kernels: 44.2 us -> 43.6 us
    pallas_call x1, Pallas kernels: 44.2 us -> 43.6 us  [body(): pl.pallas_call(kernel, out_shape=jax.ShapeDtypeStruct((BATCH_DEV * TABLES...]
where the time goes in v4:
time: 44.4 us; the launch traced here: 44.2 us
  Pallas kernels  43.6 us (98%)
  local copies, waits for them, and re-layouts  0.66 us (1%)
    pallas_call x1, Pallas kernels, body(): pl.pallas_call(kernel, out_shape=jax.ShapeDtypeStruct((BATCH_DEV * TABLES...  43.6 us

profile of v4, /device:TPU:1, one launch (start us, length us, event | category | flops | bytes accessed | tf_op | source)
XLA Modules:
  0.0 44.2 jit_solution(15030751757093229079)
XLA Ops:
  0.0 43.6 %shard_map.55 = f32[256,128]{1,0:T(8,128)S(1)} custom-call(f32[16384,1,128]{2,1,0:T(1,128)} %bitcast.16, s32[32,128]{1,0:T(8,128)} %bitcast.17, s32[32,128]{1,0:T(8,128)} %bitcast.18, s32[2,256]{1,0:T(2,128)} %hot_rows_hbm.1, s32[16,128]{1,0:T(8,128)} %bitcast.19), custom_call_target="tpu_custom_call" | custom-call | tf_op jit(solution)/shard_map/pallas_call | solution.py:309
  43.6 0.7 %copy.7 = f32[128,2,128]{2,1,0:T(2,128)} copy(f32[128,2,128]{2,1,0:T(2,128)S(1)} %bitcast.15) | data formatting | bytes 262144

commit v5 on v4

--- a/solution.py
+++ b/solution.py
@@ -13,7 +13,7 @@
 ROWS_DEV, HOT, HOT_BAG, BATCH_DEV = 8192, 256, 8, 128
 SLOTS = TABLES * CAP
 GROUP = 32
-CUTS = (60, 90)
+CUTS = (30, 85)
 
 
 def hops(offset):
@@ -167,6 +167,7 @@
     sequence = planes + corners + last
 
     def serve(first, stop):
+        ready = []
         for n in range(first, stop):
             o = sequence[n]
             px, py = at(*o)
@@ -181,11 +182,16 @@
                 asked = [idx_own[u, 0, slot] for slot in range(SLOTS)]
             for slot in range(SLOTS):
                 sbuf[n, pl.ds(slot, 1), :] = tab[asked[slot]]
-            pltpu.make_async_remote_copy(
+            copy = pltpu.make_async_remote_copy(
                 src_ref=sbuf.at[n], dst_ref=rbuf.at[n],
                 send_sem=row_ssem, recv_sem=row_rsem.at[n // 16],
                 device_id=(px, py), device_id_type=MESH,
-            ).start()
+            )
+            ready.append(copy)
+            if len(ready) > 1:
+                ready.pop(0).start()
+        for copy in ready:
+            copy.start()
 
     drain(hot_r0, h_rsem.at[0])
     hot_s0[...] = hot_own[core] + hot_r0[...]

time: 44.4 us -> 44.4 us (level)
  no operation moved by 1% of the time
where the time goes in v5:
time: 44.4 us; the launch traced here: 44.3 us
  Pallas kernels  43.6 us (98%)
  local copies, waits for them, and re-layouts  0.66 us (1%)
    pallas_call x1, Pallas kernels, body(): pl.pallas_call(kernel, out_shape=jax.ShapeDtypeStruct((BATCH_DEV * TABLES...  43.6 us

profile of v5, /device:TPU:1, one launch (start us, length us, event | category | flops | bytes accessed | tf_op | source)
XLA Modules:
  0.0 44.3 jit_solution(17841703387052283534)
XLA Ops:
  0.0 43.6 %shard_map.55 = f32[256,128]{1,0:T(8,128)S(1)} custom-call(f32[16384,1,128]{2,1,0:T(1,128)} %bitcast.16, s32[32,128]{1,0:T(8,128)} %bitcast.17, s32[32,128]{1,0:T(8,128)} %bitcast.18, s32[2,256]{1,0:T(2,128)} %hot_rows_hbm.1, s32[16,128]{1,0:T(8,128)} %bitcast.19), custom_call_target="tpu_custom_call" | custom-call | tf_op jit(solution)/shard_map/pallas_call | solution.py:315
  43.6 0.7 %copy.7 = f32[128,2,128]{2,1,0:T(2,128)} copy(f32[128,2,128]{2,1,0:T(2,128)S(1)} %bitcast.15) | data formatting | bytes 262144

commit v6 on v5

--- a/solution.py
+++ b/solution.py
@@ -14,6 +14,7 @@
 SLOTS = TABLES * CAP
 GROUP = 32
 CUTS = (30, 85)
+HEAD = 16
 
 
 def hops(offset):
@@ -39,6 +40,8 @@
     last = [o for o in every if hops(o) <= LAST]
     corners = [o for o in every if o[0] and o[2] and o[3]]
     planes = [o for o in every if o not in last and o not in corners]
+    head = [o for o in planes if o[3]][:HEAD]
+    planes = head + [o for o in planes if o not in head]
     return planes, corners, last
 
 
@@ -211,9 +214,10 @@
     own_idx = pltpu.make_async_copy(idx_mid.at[x], idx_own, self_sem)
     own_idx.start()
 
+    serve(0, HEAD)
     own_idx.wait()
 
-    serve(0, min(CUTS[0], len(planes)))
+    serve(HEAD, min(CUTS[0], len(planes)))
 
     drain(hot_r1, h_rsem.at[1])
     total = hot_r1[0]

time: 44.4 us -> 43.7 us (0.984)
  Pallas kernels: 43.6 us -> 42.8 us
    pallas_call x1, Pallas kernels: 43.6 us -> 42.8 us  [body(): pl.pallas_call(kernel, out_shape=jax.ShapeDtypeStruct((BATCH_DEV * TABLES...]
where the time goes in v6:
time: 43.7 us; the launch traced here: 43.5 us
  Pallas kernels  42.8 us (98%)
  local copies, waits for them, and re-layouts  0.66 us (2%)
    pallas_call x1, Pallas kernels, body(): pl.pallas_call(kernel, out_shape=jax.ShapeDtypeStruct((BATCH_DEV * TABLES...  42.8 us

profile of v6, /device:TPU:1, one launch (start us, length us, event | category | flops | bytes accessed | tf_op | source)
XLA Modules:
  0.0 43.5 jit_solution(16160452412904398783)
XLA Ops:
  0.0 42.8 %shard_map.55 = f32[256,128]{1,0:T(8,128)S(1)} custom-call(f32[16384,1,128]{2,1,0:T(1,128)} %bitcast.16, s32[32,128]{1,0:T(8,128)} %bitcast.17, s32[32,128]{1,0:T(8,128)} %bitcast.18, s32[2,256]{1,0:T(2,128)} %hot_rows_hbm.1, s32[16,128]{1,0:T(8,128)} %bitcast.19), custom_call_target="tpu_custom_call" | custom-call | tf_op jit(solution)/shard_map/pallas_call | solution.py:319
  42.8 0.7 %copy.7 = f32[128,2,128]{2,1,0:T(2,128)} copy(f32[128,2,128]{2,1,0:T(2,128)S(1)} %bitcast.15) | data formatting | bytes 262144
